TPU v7x, 32 devices: a whole 2x2x4 slice. The times are simulated.
32 devices in a mesh: dp: 2 (over core), seq: 4 (over y, x), tensor: 4 (over z).
Axes of the slice: x: 2, y: 2, z: 4, core: 2. Of those that a mesh axis runs over, the one named last changes fastest.
Arguments:
- tokens: bfloat16 [2, 2048, 2048], P('dp', ('seq', 'tensor')), may hold values from -6 to 6
- attn_gain: float32 [2048], replicated, may hold values from 0.5 to 1.5
- w_qkv: bfloat16 [3, 2048, 2048], P(None, None, 'tensor'), may hold values from -1 to 1
- w_out: bfloat16 [2048, 2048], P('tensor'), may hold values from -0.125 to 0.125
- mlp_gain: float32 [2048], replicated, may hold values from 0.5 to 1.5
- w_up: bfloat16 [2048, 8192], P(None, 'tensor'), may hold values from -0.125 to 0.125
- w_down: bfloat16 [8192, 2048], P('tensor'), may hold values from -0.0625 to 0.0625
- pool_gain: float32 [2048], replicated, may hold values from -8 to 8
- pool_bias: float32 [2048], replicated, may hold values from 0.5 to 5
- value_weight: float32 [2048], replicated, may hold values from -6 to 6
- valid_frames: int32 [2], replicated, may hold values from 4 to 8, as said below
Outputs:
- hidden: bfloat16 [2, 2048, 2048], P('dp', ('seq', 'tensor'))
- frame_values: float32 [2, 8], P('dp', 'seq')
- advantages: float32 [2, 8], P('dp', 'seq')
Inputs may be any that keep to these rules, and one draw needn't show every extreme that they name: `valid_frames`: at least one rollout keeps all 8 frames and at least one keeps 8 // 2 of them.
All inputs are finite; a program needn't handle non-finite values.
Results may differ from a plain program's by a relative error of at most 0.017.
Values may be sent and summed in bfloat16 or wider, within the bound.
A program may use at most 256 MiB of HBM per device.

v0:
```python
import functools

import jax
import jax.numpy as jnp
from jax import lax
from jax.experimental import pallas as pl
from jax.experimental.pallas import tpu as pltpu
from jax.sharding import PartitionSpec as P

HEAD_DIM = 128
TOK_FRAME = 256
LANES = 128
MESH = pl.DeviceIdType.MESH
F32 = jnp.float32
BF16 = jnp.bfloat16


def rms_norm(floats, gain):
    square = jnp.mean(floats * floats, axis=-1, keepdims=True)
    return (floats * lax.rsqrt(square + 1e-05) * gain).astype(BF16)


def kernel(
    tok, attn_gain, w_qkv_h, w_out_h, mlp_gain, w_up_h, w_down_h, pool_gain, pool_bias,
    value_weight, lens,
    hidden, small,
    w_qkv, w_out, w_up, w_down, ag1, ag2, query, kv, peak, total, acc, mixed, part, rs,
    after, upbuf, fsum, means,
    wsem, ag_s, ag_r, kv_s, kv_r, rs_s, rs_r, fs_s, fs_r, mn_s, mn_r,
):
    T, S, DP = (lax.axis_size("tensor"), lax.axis_size("seq"), lax.axis_size("dp"))
    z, me, roll = (lax.axis_index("tensor"), lax.axis_index("seq"), lax.axis_index("dp"))
    rows, width = tok.shape
    block = rows * T
    heads = query.shape[-1] // HEAD_DIM
    hcols = query.shape[-1]
    ff = w_up.shape[1]
    fr_dev = block // TOK_FRAME
    scale = 1.0 / HEAD_DIM**0.5
    right, left = (lax.rem(z + 1, T), lax.rem(z + T - 1, T))
    tile = 512

    loads = [
        pltpu.make_async_copy(src, dst, wsem.at[i])
        for i, (src, dst) in enumerate(
            ((w_qkv_h, w_qkv), (w_out_h, w_out), (w_up_h, w_up), (w_down_h, w_down))
        )
    ]
    for load in loads:
        load.start()

    barrier = pltpu.get_barrier_semaphore()
    for d in range(1, T):
        pl.semaphore_signal(barrier, 1, device_id={"tensor": lax.rem(z + d, T)}, device_id_type=MESH)
    peers = []
    for a in range(DP):
        for b in range(S):
            if a or b:
                peers.append({"dp": lax.rem(roll + a, DP), "seq": lax.rem(me + b, S)})
    for peer in peers:
        pl.semaphore_signal(barrier, 1, device_id=peer, device_id_type=MESH)

    ag1[z] = rms_norm(tok[...].astype(F32), attn_gain[...])
    pl.semaphore_wait(barrier, T - 1 + len(peers))

    def zcopy(src, dst, s_sem, r_sem, to):
        return pltpu.make_async_remote_copy(
            src_ref=src, dst_ref=dst, send_sem=s_sem, recv_sem=r_sem,
            device_id={"tensor": to}, device_id_type=MESH,
        )

    def gather(buf, which, first, size, process):
        def send(s, way):
            ref = buf.at[s, pl.ds(first, size)]
            return zcopy(
                ref, ref, ag_s.at[which, way, s], ag_r.at[which, s], right if way == 0 else left
            )

        def begin():
            @pl.when(z < T - 1)
            def _():
                send(z, 0).start()

            @pl.when(z > 0)
            def _():
                send(z, 1).start()

            process(z)

        def step(k):
            a, b = (z - k, z + k)

            @pl.when(a >= 0)
            def _():
                send(a, 0).wait_recv()

                @pl.when(z < T - 1)
                def _():
                    send(a, 0).start()

            @pl.when(b < T)
            def _():
                send(b, 1).wait_recv()

                @pl.when(z > 0)
                def _():
                    send(b, 1).start()

            @pl.when(a >= 0)
            def _():
                process(a)

            @pl.when(b < T)
            def _():
                process(b)

        def drain():
            for s in range(T):

                @pl.when((s <= z) & (z < T - 1))
                def _():
                    send(s, 0).wait_send()

                @pl.when((s >= z) & (z > 0))
                def _():
                    send(s, 1).wait_send()

        return (begin, step, drain)

    def run_gather(begin, step, drain):
        begin()

        def body(k, carry):
            step(k)
            return carry

        lax.fori_loop(1, T, body, 0)
        drain()

    def scatter(buf, which, first, size):
        span = pl.ds(first, size)

        def send(d, way):
            ref = buf.at[way, d, span]
            return zcopy(
                ref, ref, rs_s.at[which, way, d], rs_r.at[which, way, d],
                right if way == 0 else left,
            )

        def move(d, way, opens):
            @pl.when(opens)
            def _():
                buf[way, d, span] = part[d, span]

            @pl.when(jnp.logical_not(opens))
            def _():
                send(d, way).wait_recv()
                buf[way, d, span] = (
                    buf[way, d, span].astype(F32) + part[d, span].astype(F32)
                ).astype(BF16)

            send(d, way).start()

        def hop(k):
            d = T - 1 - k

            @pl.when(z < d)
            def _():
                move(d, 0, z == 0)

            @pl.when(z > k)
            def _():
                move(k, 1, z == T - 1)

        def finish():
            after[span] = after[span] + part[z, span].astype(F32)

            @pl.when(z > 0)
            def _():
                send(z, 0).wait_recv()
                after[span] = after[span] + buf[0, z, span].astype(F32)

            @pl.when(z < T - 1)
            def _():
                send(z, 1).wait_recv()
                after[span] = after[span] + buf[1, z, span].astype(F32)

        def drain():
            for d in range(T):

                @pl.when(z < d)
                def _(d=d):
                    send(d, 0).wait_send()

                @pl.when(z > d)
                def _(d=d):
                    send(d, 1).wait_send()

        return (hop, finish, drain)

    def kv_send(d, s):
        return pltpu.make_async_remote_copy(
            src_ref=kv.at[me, s], dst_ref=kv.at[me, s], send_sem=kv_s.at[d, s],
            recv_sem=kv_r.at[me, s], device_id={"seq": lax.rem(me + d, S)}, device_id_type=MESH,
        )

    def project(s):
        x = ag1[s]
        kv[me, s, 0] = jnp.dot(x, w_qkv[1], preferred_element_type=F32).astype(BF16)
        kv[me, s, 1] = jnp.dot(x, w_qkv[2], preferred_element_type=F32).astype(BF16)
        for d in range(1, S):

            @pl.when(me + d < S)
            def _(d=d):
                kv_send(d, s).start()

        query[s] = jnp.dot(x, w_qkv[0], preferred_element_type=F32).astype(BF16)

    loads[0].wait()
    run_gather(*gather(ag1, 0, 0, rows, project))

    peak[...] = jnp.full_like(peak, -1e30)
    total[...] = jnp.zeros_like(total)
    acc[...] = jnp.zeros_like(acc)
    length = lens[pl.ds(roll, 1)][0, 0:1, 0:1].astype(jnp.int32)

    def attend(j):
        q_frame = me * fr_dev + lax.broadcasted_iota(jnp.int32, (block, 1), 0) // TOK_FRAME
        k_frame = j * fr_dev + lax.broadcasted_iota(jnp.int32, (1, block), 1) // TOK_FRAME
        allowed = (k_frame <= q_frame) & (k_frame < length)

        def head(h, carry):
            cols = pl.ds(pl.multiple_of(h * HEAD_DIM, HEAD_DIM), HEAD_DIM)
            q = query[:, :, cols].reshape(block, HEAD_DIM)
            k = kv[j, :, 0, :, cols].reshape(block, HEAD_DIM)
            v = kv[j, :, 1, :, cols].reshape(block, HEAD_DIM)
            scores = lax.dot_general(q, k, (((1,), (1,)), ((), ())), preferred_element_type=F32)
            scores = jnp.where(allowed, scores * scale, -1e30)
            old = peak[h]
            new = jnp.maximum(old, jnp.max(scores, axis=-1, keepdims=True))
            weights = jnp.where(allowed, jnp.exp(scores - new), 0.0)
            shrink = jnp.exp(old - new)
            peak[h] = new
            total[h] = total[h] * shrink + jnp.sum(weights, axis=-1, keepdims=True)
            acc[h] = acc[h] * shrink + jnp.dot(weights.astype(BF16), v, preferred_element_type=F32)
            return carry

        lax.fori_loop(0, heads, head, 0)

    attend(me)

    def earlier(d, carry):
        j = me - d

        @pl.when(j >= 0)
        def _():
            for s in range(T):
                pltpu.make_async_remote_copy(
                    src_ref=kv.at[j, s], dst_ref=kv.at[j, s], send_sem=kv_s.at[0, s],
                    recv_sem=kv_r.at[j, s], device_id={"seq": lax.rem(me + 1, S)},
                    device_id_type=MESH,
                ).wait_recv()
            attend(j)

        return carry

    lax.fori_loop(1, S, earlier, 0)
    for h in range(heads):
        mixed[:, h * HEAD_DIM : (h + 1) * HEAD_DIM] = (acc[h] / total[h]).astype(BF16)

    loads[1].wait()

    def out_tile(n, carry):
        cols = pl.ds(pl.multiple_of(n * tile, tile), tile)
        res = jnp.dot(mixed[...], w_out[:, cols], preferred_element_type=F32)
        part[:, :, cols] = res.astype(BF16).reshape(T, rows, tile)
        return carry

    lax.fori_loop(0, width // tile, out_tile, 0)
    after[...] = tok[...].astype(F32)
    loads[2].wait()
    loads[3].wait()

    def feed(s):
        def up_tile(n, carry):
            cols = pl.ds(pl.multiple_of(n * tile, tile), tile)
            res = jnp.dot(ag2[s], w_up[:, cols], preferred_element_type=F32)
            upbuf[:, cols] = jax.nn.gelu(res, approximate=True).astype(BF16)
            return carry

        lax.fori_loop(0, ff // tile, up_tile, 0)

        def down_tile(n, carry):
            cols = pl.ds(pl.multiple_of(n * tile, tile), tile)
            res = jnp.dot(upbuf[...], w_down[:, cols], preferred_element_type=F32)
            part[s, :, cols] = res.astype(BF16)
            return carry

        lax.fori_loop(0, width // tile, down_tile, 0)

    half = rows // 2
    hop0, finish0, drain0 = scatter(rs, 0, 0, half)
    hop1, finish1, drain1 = scatter(rs, 1, half, half)
    begin0, step0, settle0 = gather(ag2, 1, 0, half, lambda s: None)

    def renorm(first):
        span = pl.ds(first, half)
        rounded = after[span].astype(BF16).astype(F32)
        after[span] = rounded
        ag2[z, span] = rms_norm(rounded, mlp_gain[...])

    for k in range(T - 1):
        hop0(k)
    hop1(0)
    finish0()
    renorm(0)
    begin0()
    for k in range(1, T):
        if k < T - 1:
            hop1(k)
        step0(k)
    finish1()
    drain0()
    drain1()
    renorm(half)
    run_gather(*gather(ag2, 2, half, half, feed))
    settle0()
    hop2, finish2, drain2 = scatter(rs, 2, 0, rows)
    for k in range(T - 1):
        hop2(k)
    finish2()
    drain2()
    out = after[...].astype(BF16)
    hidden[...] = out
    sums = jnp.sum(out.astype(F32), axis=0, keepdims=True)
    chunks = width // LANES
    for c in range(chunks):
        fsum[z, c : c + 1, :] = sums[:, c * LANES : (c + 1) * LANES]

    def fs_send(d):
        return zcopy(fsum.at[z], fsum.at[z], fs_s.at[d], fs_r.at[z], lax.rem(z + d, T))

    for d in range(1, T):
        fs_send(d).start()
    for d in range(1, T):
        o = lax.rem(z + T - d, T)
        zcopy(fsum.at[o], fsum.at[o], fs_s.at[0], fs_r.at[o], right).wait_recv()
    per = T // fr_dev
    for f in range(fr_dev):
        m = fsum[f * per]
        for s in range(f * per + 1, (f + 1) * per):
            m = m + fsum[s]
        means[roll, me, f] = m / TOK_FRAME

    def mn_send(i, peer):
        return pltpu.make_async_remote_copy(
            src_ref=means.at[roll, me], dst_ref=means.at[roll, me], send_sem=mn_s.at[i],
            recv_sem=mn_r.at[roll, me], device_id=peer, device_id_type=MESH,
        )

    for i, peer in enumerate(peers):
        mn_send(i, peer).start()
    for a in range(DP):
        for b in range(S):
            if a or b:
                ra, sb = (lax.rem(roll + a, DP), lax.rem(me + b, S))
                pltpu.make_async_remote_copy(
                    src_ref=means.at[ra, sb], dst_ref=means.at[ra, sb], send_sem=mn_s.at[0],
                    recv_sem=mn_r.at[ra, sb], device_id=peers[0], device_id_type=MESH,
                ).wait_recv()

    lane = lax.broadcasted_iota(jnp.int32, (1, LANES), 1)
    values, gaps, valids = ([], [], [])
    for r in range(DP):
        span = lens[r]

        def frame(f, carry):
            state, vec = carry
            m = means[r, f // fr_dev, lax.rem(f, fr_dev)]
            gate = jax.nn.sigmoid(m * pool_gain[...] + pool_bias[...])
            new = gate * state + (1.0 - gate) * m
            state = jnp.where(span > f.astype(F32), new, state)
            dot = jnp.sum(jnp.sum(state * value_weight[...], axis=1, keepdims=True), axis=0, keepdims=True)
            return (state, jnp.where(lane == f, dot, vec))

        zero = (jnp.zeros((chunks, LANES), F32), jnp.zeros((1, LANES), F32))
        _, vec = lax.fori_loop(0, S * fr_dev, frame, zero)
        length_r = span[0:1].astype(jnp.int32)
        ok = lane < length_r
        vec = jnp.where(ok, vec, 0.0)
        reward = jnp.sum(jnp.where(lane == length_r - 1, vec, 0.0), axis=1, keepdims=True)
        values.append(vec)
        valids.append(ok)
        gaps.append(jnp.where(ok, reward - vec, 0.0))
    count = sum(lens[r][0:1, 0:1] for r in range(DP))
    mean = sum(jnp.sum(g, axis=1, keepdims=True) for g in gaps) / count
    centered = [jnp.where(ok, g - mean, 0.0) for ok, g in zip(valids, gaps)]
    variance = sum(jnp.sum(c * c, axis=1, keepdims=True) for c in centered) / count
    for r in range(DP):
        small[r : r + 1, :] = values[r]
        small[DP + r : DP + r + 1, :] = jnp.where(
            valids[r], centered[r] * lax.rsqrt(variance + 1e-05), 0.0
        )

    for d in range(1, T):
        fs_send(d).wait_send()
    for i, peer in enumerate(peers):
        mn_send(i, peer).wait_send()
    for d in range(1, S):

        @pl.when(me + d < S)
        def _(d=d):
            for s in range(T):
                kv_send(d, s).wait_send()


def local(
    tokens, attn_gain, w_qkv, w_out, mlp_gain, w_up, w_down, pool_gain, pool_bias, value_weight,
    valid_frames,
):
    T, S, DP = (lax.axis_size("tensor"), lax.axis_size("seq"), lax.axis_size("dp"))
    rows, width = tokens.shape[1:]
    block = rows * T
    fr_dev = block // TOK_FRAME
    chunks = width // LANES
    hcols = w_qkv.shape[2]
    heads = hcols // HEAD_DIM
    assert TOK_FRAME % rows == 0 and S * fr_dev <= LANES
    lens = jnp.broadcast_to(valid_frames.astype(F32)[:, None, None], (DP, chunks, LANES))
    vm = pl.BlockSpec(memory_space=pltpu.VMEM)
    hbm = pl.BlockSpec(memory_space=pl.ANY)
    dma = pltpu.SemaphoreType.DMA
    small_rows = -(-2 * DP // 8) * 8
    hidden, small = pl.pallas_call(
        kernel,
        out_shape=(
            jax.ShapeDtypeStruct((rows, width), BF16),
            jax.ShapeDtypeStruct((small_rows, LANES), F32),
        ),
        in_specs=[vm, vm, hbm, hbm, vm, hbm, hbm, vm, vm, vm, vm],
        out_specs=(vm, vm),
        scratch_shapes=[
            pltpu.VMEM(w_qkv.shape, BF16),
            pltpu.VMEM(w_out.shape, BF16),
            pltpu.VMEM(w_up.shape, BF16),
            pltpu.VMEM(w_down.shape, BF16),
            pltpu.VMEM((T, rows, width), BF16),
            pltpu.VMEM((T, rows, width), BF16),
            pltpu.VMEM((T, rows, hcols), BF16),
            pltpu.VMEM((S, T, 2, rows, hcols), BF16),
            pltpu.VMEM((heads, block, 1), F32),
            pltpu.VMEM((heads, block, 1), F32),
            pltpu.VMEM((heads, block, HEAD_DIM), F32),
            pltpu.VMEM((block, hcols), BF16),
            pltpu.VMEM((T, rows, width), BF16),
            pltpu.VMEM((2, T, rows, width), BF16),
            pltpu.VMEM((rows, width), F32),
            pltpu.VMEM((rows, w_up.shape[1]), BF16),
            pltpu.VMEM((T, chunks, LANES), F32),
            pltpu.VMEM((DP, S, fr_dev, chunks, LANES), F32),
            dma((4,)),
            dma((3, 2, T)),
            dma((3, T)),
            dma((S, T)),
            dma((S, T)),
            dma((3, 2, T)),
            dma((3, 2, T)),
            dma((T,)),
            dma((T,)),
            dma((DP * S,)),
            dma((DP, S)),
        ],
        compiler_params=pltpu.CompilerParams(
            collective_id=0, has_side_effects=True, vmem_limit_bytes=67043328
        ),
    )(
        tokens[0],
        attn_gain[None],
        w_qkv,
        w_out,
        mlp_gain[None],
        w_up,
        w_down,
        pool_gain.reshape(chunks, LANES),
        pool_bias.reshape(chunks, LANES),
        value_weight.reshape(chunks, LANES),
        lens,
    )
    roll, seq = (lax.axis_index("dp"), lax.axis_index("seq"))
    values = lax.dynamic_slice(small, (roll, seq * fr_dev), (1, fr_dev))
    advantages = lax.dynamic_slice(small, (DP + roll, seq * fr_dev), (1, fr_dev))
    return (hidden[None], values, advantages)


def solution(mesh):
    in_specs = (
        P("dp", ("seq", "tensor"), None),
        P(),
        P(None, None, "tensor"),
        P("tensor", None),
        P(),
        P(None, "tensor"),
        P("tensor", None),
        P(),
        P(),
        P(),
        P(),
    )
    out_specs = (P("dp", ("seq", "tensor"), None), P("dp", "seq"), P("dp", "seq"))
    return jax.shard_map(local, mesh=mesh, in_specs=in_specs, out_specs=out_specs, check_vma=False)
```

profile of v0, /device:TPU:0, one launch (start us, length us, event | category | flops | bytes accessed | tf_op | source)
XLA Modules:
  0.0 210.4 jit_solution(8107530327618281792)
XLA Ops:
  0.6 0.7 convert_element_type.3
  1.3 0.7 broadcast_in_dim.17.lens
  2.0 205.2 %shard_map.130 = (bf16[128,2048]{1,0:T(8,128)(2,1)}, f32[8,128]{1,0:T(8,128)}) custom-call(bf16[128,2048]{1,0:T(8,128)(2,1)} %bitcast.8, f32[1,2048]{1,0:T(1,128)} %bitcast.9, bf16[3,2048,512]{2,1,0:T(8,128)(2,1)} %w_qkv_h.1, bf16[512,2048]{1,0:T(8,128)(2,1)} %w_out_h.1, f32[1,2048]{1,0:T(1,128)} %bitcast.10, bf16[2048,2048]{1,0:T(8,128)(2,1)} %w_up_h.1, ...), custom_call_target="tpu_custom_call" | custom-call | tf_op jit(solution)/shard_map/pallas_call | solution.py:434
  207.2 1.4 fusion
  208.5 1.9 copy.15
where the time goes:
time: 211 us; the launch traced here: 210 us
  Pallas kernels  205 us (97%)
  local copies, waits for them, and re-layouts  3.91 us (2%)
    pallas_call x1, Pallas kernels, local(): pl.pallas_call(kernel, out_shape=(jax.ShapeDtypeStruct((rows, width), BF1...  205 us

commit v1 on v0

v1 whole, which is shorter than its diff:
```python
import math

import jax
import jax.numpy as jnp
from jax import lax
from jax.experimental import pallas as pl
from jax.experimental.pallas import tpu as pltpu
from jax.sharding import PartitionSpec as P

HEAD_DIM = 128
TOK_FRAME = 256
LANES = 128
CHUNKS = 4
HALVES = 2
LAG = 2
MESH = pl.DeviceIdType.MESH
F32 = jnp.float32
BF16 = jnp.bfloat16


def rms_norm(floats, gain):
    square = jnp.mean(floats * floats, axis=-1, keepdims=True)
    return (floats * lax.rsqrt(square + 1e-05) * gain).astype(BF16)


def loop(n, body):
    def step(i, carry):
        body(i)
        return carry

    lax.fori_loop(0, n, step, 0)


def kernel(
    tok, attn_gain, w_qkv_h, w_out_h, mlp_gain, w_up_h, w_down_h, pool_gain, pool_bias,
    value_weight, lens,
    hidden, small,
    w_qkv, w_out, w_up, w_down, ag1, query, kv, peak, total, acc, mixed, aft, own, normed,
    upbuf, part, rs, fsum, means,
    wsem, ag_s, ag_r, kv_s, kv_r, kvr_s, wz_s, wp_s, wr_s, wd_s, wo_r, mx_s, mx_r, rs_s, rs_r,
    fs_s, fs_r, mn_s, mn_r,
):
    T, S, DP = (lax.axis_size("tensor"), lax.axis_size("seq"), lax.axis_size("dp"))
    z, me, roll = (lax.axis_index("tensor"), lax.axis_index("seq"), lax.axis_index("dp"))
    C, cr, width = tok.shape
    rows = C * cr
    block = rows * T
    qc = T * cr
    NH = HALVES
    per_half = C // NH
    hr = rows // NH
    hcols = query.shape[-1]
    heads = hcols // HEAD_DIM
    ff = w_up.shape[1]
    fr_dev = block // TOK_FRAME
    square = S == 4
    right, left = (lax.rem(z + 1, T), lax.rem(z + T - 1, T))
    tile = 1024
    ends = (z == 0) | (z == T - 1)
    mine = roll * S + me
    other = lax.rem(roll + 1, DP)

    loads = [
        pltpu.make_async_copy(src, dst, wsem.at[i])
        for i, (src, dst) in enumerate(
            ((w_qkv_h, w_qkv), (w_out_h, w_out.at[z]), (w_up_h, w_up), (w_down_h, w_down))
        )
    ]
    for load in loads:
        load.start()

    barrier = pltpu.get_barrier_semaphore()
    for d in range(1, T):
        pl.semaphore_signal(barrier, 1, device_id={"tensor": lax.rem(z + d, T)}, device_id_type=MESH)
    peers = []
    for a in range(DP):
        for b in range(S):
            if a or b:
                peers.append({"dp": lax.rem(roll + a, DP), "seq": lax.rem(me + b, S)})
    for peer in peers:
        pl.semaphore_signal(barrier, 1, device_id=peer, device_id_type=MESH)
    pl.semaphore_wait(barrier, T - 1 + len(peers))

    def rcopy(src, dst, s_sem, r_sem, to):
        return pltpu.make_async_remote_copy(
            src_ref=src, dst_ref=dst, send_sem=s_sem, recv_sem=r_sem, device_id=to,
            device_id_type=MESH,
        )

    def zcopy(src, dst, s_sem, r_sem, to):
        return rcopy(src, dst, s_sem, r_sem, {"tensor": to})

    def toward(way):
        return right if way == 0 else left

    def tok_send(s, h, way, src=None):
        ref = ag1.at[s, pl.ds(h * per_half, per_half)]
        return zcopy(ref if src is None else src, ref, ag_s.at[way, s, h], ag_r.at[s, h], toward(way))

    def own_send(h, way):
        return tok_send(z, h, way, tok.at[pl.ds(h * per_half, per_half)])

    for h in range(NH):

        @pl.when(z < T - 1)
        def _(h=h):
            own_send(h, 0).start()

        @pl.when(z > 0)
        def _(h=h):
            own_send(h, 1).start()

    def arrival(u):
        near = jnp.minimum(z, T - 1 - z)
        paired = u <= 2 * near
        k = jnp.where(paired, lax.div(u + 1, 2), u - near)
        odd = lax.rem(u, 2)
        longer = jnp.where(z > T - 1 - z, 1, 0)
        from_left = jnp.where(paired, odd, longer)
        return (jnp.where(from_left == 1, z - k, z + k), from_left)

    def kv_copy(j, s, h, i, sem, to):
        ref = kv.at[j, s, h, i]
        return rcopy(ref, ref, sem, kv_r.at[j, s, h, i], {"seq": to})

    def kv_send(d, s, h, i):
        return kv_copy(me, s, h, i, kv_s.at[d, s, h, i], lax.rem(me + d, S))

    def kv_direct(d):
        cond = me + d < S
        if square and d == 3:
            cond = cond & (me != 0)
        if square and d == 1:
            cond = cond & (me != 1)
        return cond

    relay_from = jnp.where(me == 3, 1, 0)
    relay_to = jnp.where(me == 3, 2, 3)

    def relays(i):
        return (me == 3) | (me == 1 + i)

    def kv_relay_copy(s, h, i):
        return kv_copy(relay_from, s, h, i, kvr_s.at[s, h, i], relay_to)

    def kv_relay(n):
        if square:
            s, _ = arrival(lax.div(n, NH))
            h = lax.rem(n, NH)
            for i in range(2):

                @pl.when(relays(i))
                def _(i=i):
                    copy = kv_relay_copy(s, h, i)
                    copy.wait_recv()
                    copy.start()

    def kv_rest(n):
        s, h = (lax.div(n, NH), lax.rem(n, NH))

        def source(j, carry):
            for i in range(2):
                cond = j < me
                if square:
                    cond = cond & jnp.logical_not(relays(i) & (j == relay_from))

                @pl.when(cond)
                def _(i=i):
                    kv_copy(j, s, h, i, kv_s.at[0, s, h, i], lax.rem(me + 1, S)).wait_recv()

            return carry

        lax.fori_loop(0, S - 1, source, 0)

    def project(s, h):
        floats = ag1[s, pl.ds(h * per_half, per_half)].astype(F32).reshape(hr, width)
        x = rms_norm(floats, attn_gain[...])
        for i in range(2):
            kv[me, s, h, i] = jnp.dot(x, w_qkv[1 + i], preferred_element_type=F32).astype(BF16)
            for d in range(1, S):

                @pl.when(kv_direct(d))
                def _(d=d, i=i):
                    kv_send(d, s, h, i).start()

        q = jnp.dot(x, w_qkv[0], preferred_element_type=F32).astype(BF16)
        query[s, pl.ds(h * per_half, per_half)] = q.reshape(per_half, cr, hcols)

    def w_ref(zz, r, f):
        half = w_out.shape[2] // 2
        return w_out.at[zz, r, pl.ds(f * half, half)]

    def w_copy(zz, r, f, sem, to):
        ref = w_ref(zz, r, f)
        return rcopy(ref, ref, sem, wo_r.at[zz, r, f], to)

    def wz_send(zz, f, way):
        return w_copy(zz, mine, f, wz_s.at[way, zz, f], {"tensor": toward(way)})

    flip_x = me + 1 - 2 * lax.rem(me, 2)
    flip_y = lax.rem(me + 2, 4)
    flip_d = flip_x + 2 - 4 * lax.div(flip_x, 2)

    def plane_targets():
        if square:
            return [flip_x, flip_y]
        return [lax.rem(me + d, S) for d in range(1, S)]

    def plane_sends(zz, f):
        return [
            w_copy(zz, mine, f, wp_s.at[n, zz, f], {"seq": to})
            for n, to in enumerate(plane_targets())
        ]

    def die_send(zz, b, f):
        return w_copy(zz, roll * S + b, f, wd_s.at[b, zz, f], {"dp": other})

    def w_relay(zz, axis):
        if axis == 0:
            return w_copy(zz, roll * S + flip_x, 0, wr_s.at[zz, 0], {"seq": flip_y})
        return w_copy(zz, roll * S + flip_y, 1, wr_s.at[zz, 1], {"seq": flip_x})

    def w_begin():
        for f in range(2):

            @pl.when(z < T - 1)
            def _(f=f):
                wz_send(z, f, 0).start()

            @pl.when(z > 0)
            def _(f=f):
                wz_send(z, f, 1).start()

    def sides(k):
        return ((z - k, z - k >= 0, 0, z < T - 1), (z + k, z + k < T, 1, z > 0))

    def w_step(k):
        for zz, here, way, more in sides(k):

            @pl.when(here)
            def _(zz=zz, way=way, more=more):
                for f in range(2):
                    wz_send(zz, f, way).wait_recv()

                    @pl.when(more)
                    def _(f=f):
                        wz_send(zz, f, way).start()

                    for copy in plane_sends(zz, f):
                        copy.start()
                    die_send(zz, me, f).start()

    def w_spread(k):
        for zz, here, _, _ in sides(k):

            @pl.when(here)
            def _(zz=zz):
                if square:
                    for axis, b in ((0, flip_x), (1, flip_y)):
                        for f in range(2):
                            die_send(zz, b, f).wait_recv()
                        w_relay(zz, axis).start()
                        for f in range(2):
                            die_send(zz, b, f).start()
                else:
                    for d in range(1, S):
                        b = lax.rem(me + d, S)
                        for f in range(2):
                            die_send(zz, b, f).wait_recv()
                            die_send(zz, b, f).start()

    def w_diagonal(k):
        if square:
            for zz, here, _, _ in sides(k):

                @pl.when(here)
                def _(zz=zz):
                    for f in range(2):
                        copy = die_send(zz, flip_d, f)
                        copy.wait_recv()
                        copy.start()

    def w_finish(k):
        for zz, here, _, _ in sides(k):

            @pl.when(here)
            def _(zz=zz):
                def piece(b, carry):
                    for f in range(2):
                        w_copy(
                            zz, other * S + b, f, wd_s.at[b, zz, f], {"dp": other}
                        ).wait_recv()
                    return carry

                lax.fori_loop(0, S, piece, 0)

    def w_drain(k):
        for zz, here, way, more in sides(k):

            @pl.when(here)
            def _(zz=zz, way=way, more=more):
                for f in range(2):

                    @pl.when(more)
                    def _(f=f):
                        wz_send(zz, f, way).wait_send()

                    for copy in plane_sends(zz, f):
                        copy.wait_send()
                    if square:
                        w_relay(zz, f).wait_send()

                def piece(b, carry):
                    for f in range(2):
                        die_send(zz, b, f).wait_send()
                    return carry

                lax.fori_loop(0, S, piece, 0)

    ag1[z] = tok[...]
    loads[0].wait()

    def gather(i):
        u, h = (lax.div(i, NH), lax.rem(i, NH))
        s, from_left = arrival(u)

        @pl.when(u > 0)
        def _():
            tok_send(s, h, 0).wait_recv()

            @pl.when((from_left == 1) & (z < T - 1))
            def _():
                tok_send(s, h, 0).start()

            @pl.when((from_left == 0) & (z > 0))
            def _():
                tok_send(s, h, 1).start()

        @pl.when(i == NH)
        def _():
            loads[1].wait()

            @pl.when(ends)
            def _():
                w_begin()

        project(s, h)

        @pl.when(i >= LAG)
        def _():
            kv_relay(i - LAG)

    loop(T * NH, gather)

    @pl.when(jnp.logical_not(ends))
    def _():
        w_begin()

    length = lens[pl.ds(roll, 1)][0, 0:1, 0:1].astype(jnp.int32)
    to_bits = math.log2(math.e) / HEAD_DIM**0.5

    def attend(c):
        peak[...] = jnp.full_like(peak, -1e30)
        total[...] = jnp.zeros_like(total)
        acc[...] = jnp.zeros_like(acc)
        q_row = lax.div(lax.broadcasted_iota(jnp.int32, (fr_dev, 1, qc), 2), cr) * rows
        q_frame = me * fr_dev + lax.div(q_row, TOK_FRAME)
        k_local = lax.broadcasted_iota(jnp.int32, (fr_dev, 1, qc), 0)

        def against(j, carry):
            k_frame = j * fr_dev + k_local
            bias = jnp.where((k_frame <= q_frame) & (k_frame < length), 0.0, -1e30)
            for h in range(heads):
                cols = slice(h * HEAD_DIM, (h + 1) * HEAD_DIM)
                q = query[:, c, :, cols].reshape(qc, HEAD_DIM)
                k = kv[j, :, :, 0, :, cols].reshape(block, HEAD_DIM)
                v = kv[j, :, :, 1, :, cols].reshape(block, HEAD_DIM)
                s = lax.dot_general(k, q, (((1,), (1,)), ((), ())), preferred_element_type=F32)
                s = s.reshape(fr_dev, TOK_FRAME, qc) * to_bits + bias
                s = s.reshape(block, qc)
                old = peak[h]
                new = jnp.maximum(old, jnp.max(s, axis=0, keepdims=True))
                weights = jnp.exp2(s - new)
                shrink = jnp.exp2(old - new)
                peak[h] = new
                total[h] = total[h] * shrink + jnp.sum(weights, axis=0, keepdims=True)
                acc[h] = acc[h] * shrink + lax.dot_general(
                    v, weights.astype(BF16), (((0,), (0,)), ((), ())), preferred_element_type=F32
                )
            return carry

        lax.fori_loop(0, me + 1, against, 0)
        for h in range(heads):
            cols = slice(h * HEAD_DIM, (h + 1) * HEAD_DIM)
            mixed[c, z, :, cols] = jnp.transpose(acc[h] / total[h]).astype(BF16)

    def mx_send(c, s, way):
        ref = mixed.at[c, s]
        return zcopy(ref, ref, mx_s.at[way, c, s], mx_r.at[c, s], toward(way))

    def mx_begin(c):
        @pl.when(z < T - 1)
        def _():
            mx_send(c, z, 0).start()

        @pl.when(z > 0)
        def _():
            mx_send(c, z, 1).start()

    def mx_step(c, k):
        for s, here, way, more in sides(k):

            @pl.when(here)
            def _(s=s, way=way, more=more):
                copy = mx_send(c, s, way)
                copy.wait_recv()

                @pl.when(more)
                def _():
                    copy.start()

    def rs_send(c, d, way, opens):
        src = part.at[c, d] if opens else rs.at[c, way, d]
        return zcopy(src, rs.at[c, way, d], rs_s.at[way, c, d], rs_r.at[way, c, d], toward(way))

    def rs_open(c):
        for i in range(T - 1):

            @pl.when((z == 0) & (T - 1 - i > z))
            def _(i=i):
                rs_send(c, T - 1 - i, 0, True).start()

            @pl.when((z == T - 1) & (i < z))
            def _(i=i):
                rs_send(c, i, 1, True).start()

    def rs_pass(c, w, i):
        for d, way, here in (
            (T - 1 - i, 0, (z == w) & (T - 1 - i > z)),
            (i, 1, (T - 1 - z == w) & (i < z)),
        ):

            @pl.when(here)
            def _(d=d, way=way):
                copy = rs_send(c, d, way, False)
                copy.wait_recv()
                rs[c, way, d] = (rs[c, way, d].astype(F32) + part[c, d].astype(F32)).astype(BF16)
                copy.start()

    def rs_finish(c):
        own[c] = own[c] + part[c, z].astype(F32)

        @pl.when(z > 0)
        def _():
            rs_send(c, z, 0, False).wait_recv()
            own[c] = own[c] + rs[c, 0, z].astype(F32)

        @pl.when(z < T - 1)
        def _():
            rs_send(c, z, 1, False).wait_recv()
            own[c] = own[c] + rs[c, 1, z].astype(F32)

        hidden[c] = own[c].astype(BF16)

    passes = [(w, i) for w in range(1, T - 1) for i in range(T - 1 - w)]

    def project_out(c):
        lhs = jnp.concatenate([mixed[c, s] for s in range(T)], axis=1)

        def cols_of(n):
            cols = pl.ds(pl.multiple_of(n * tile, tile), tile)
            w = w_out[:, :, :, cols].reshape(T * hcols, tile)
            res = jnp.dot(lhs, w, preferred_element_type=F32)
            res = res + ag1[:, c, :, cols].astype(F32).reshape(qc, tile)
            aft[:, :, cols] = res.astype(BF16).reshape(T, cr, tile)

        loop(width // tile, cols_of)
        normed[...] = rms_norm(aft[...].astype(F32).reshape(qc, width), mlp_gain[...])
        own[c] = aft[z].astype(F32)

    def feed_up():
        def cols_of(n):
            cols = pl.ds(pl.multiple_of(n * tile, tile), tile)
            res = jnp.dot(normed[...], w_up[:, cols], preferred_element_type=F32)
            upbuf[:, cols] = jax.nn.gelu(res, approximate=True).astype(BF16)

        loop(ff // tile, cols_of)

    def feed_down(c):
        def cols_of(n):
            cols = pl.ds(pl.multiple_of(n * tile, tile), tile)
            res = jnp.dot(upbuf[...], w_down[:, cols], preferred_element_type=F32)
            part[c, :, :, cols] = res.astype(BF16).reshape(T, cr, tile)

        loop(width // tile, cols_of)

    w_step(1)
    for n in range(T * NH - LAG, T * NH):
        kv_relay(jnp.int32(n))
    loop(T * NH, kv_rest)
    w_step(2)

    def mix(c):
        attend(c)
        mx_begin(c)

        @pl.when(c == 0)
        def _():
            for k in range(3, T):
                w_step(k)

        @pl.when(c == 1)
        def _():
            w_spread(1)

        @pl.when(c == 2)
        def _():
            w_spread(2)
            w_diagonal(1)

    loop(C, mix)
    for k in range(3, T):
        w_spread(k)
    for k in range(2, T):
        w_diagonal(k)
    loads[2].wait()
    loads[3].wait()

    def chunk(c):
        for k in range(1, T):
            mx_step(c, k)
            for w, i in passes[k - 1 : k]:

                @pl.when(c > 0)
                def _(w=w, i=i):
                    rs_pass(c - 1, w, i)

        @pl.when(c == 0)
        def _():
            for k in range(1, T):
                w_finish(k)

        project_out(c)
        for w, i in passes[T - 1 :]:

            @pl.when(c > 0)
            def _(w=w, i=i):
                rs_pass(c - 1, w, i)

        feed_up()
        feed_down(c)
        rs_open(c)

        @pl.when(c > 0)
        def _():
            rs_finish(c - 1)

    loop(C, chunk)
    for w, i in passes:
        rs_pass(C - 1, w, i)
    rs_finish(C - 1)

    out = hidden[...].astype(F32).reshape(rows, width)
    sums = jnp.sum(out, axis=0, keepdims=True)
    chunks = width // LANES
    for c in range(chunks):
        fsum[z, c : c + 1, :] = sums[:, c * LANES : (c + 1) * LANES]

    def fs_send(d):
        return zcopy(fsum.at[z], fsum.at[z], fs_s.at[d], fs_r.at[z], lax.rem(z + d, T))

    for d in range(1, T):
        fs_send(d).start()
    for d in range(1, T):
        o = lax.rem(z + T - d, T)
        zcopy(fsum.at[o], fsum.at[o], fs_s.at[0], fs_r.at[o], right).wait_recv()
    per = T // fr_dev
    for f in range(fr_dev):
        m = fsum[f * per]
        for s in range(f * per + 1, (f + 1) * per):
            m = m + fsum[s]
        means[roll, me, f] = m / TOK_FRAME

    def mn_send(i, peer):
        return rcopy(means.at[roll, me], means.at[roll, me], mn_s.at[i], mn_r.at[roll, me], peer)

    for i, peer in enumerate(peers):
        mn_send(i, peer).start()
    for a in range(DP):
        for b in range(S):
            if a or b:
                ra, sb = (lax.rem(roll + a, DP), lax.rem(me + b, S))
                rcopy(
                    means.at[ra, sb], means.at[ra, sb], mn_s.at[0], mn_r.at[ra, sb], peers[0]
                ).wait_recv()

    lane = lax.broadcasted_iota(jnp.int32, (1, LANES), 1)
    values, gaps, valids = ([], [], [])
    for r in range(DP):
        span = lens[r]

        def frame(f, carry):
            state, vec = carry
            m = means[r, f // fr_dev, lax.rem(f, fr_dev)]
            gate = jax.nn.sigmoid(m * pool_gain[...] + pool_bias[...])
            new = gate * state + (1.0 - gate) * m
            state = jnp.where(span > f.astype(F32), new, state)
            dot = jnp.sum(jnp.sum(state * value_weight[...], axis=1, keepdims=True), axis=0, keepdims=True)
            return (state, jnp.where(lane == f, dot, vec))

        zero = (jnp.zeros((chunks, LANES), F32), jnp.zeros((1, LANES), F32))
        _, vec = lax.fori_loop(0, S * fr_dev, frame, zero)
        length_r = span[0:1].astype(jnp.int32)
        ok = lane < length_r
        vec = jnp.where(ok, vec, 0.0)
        reward = jnp.sum(jnp.where(lane == length_r - 1, vec, 0.0), axis=1, keepdims=True)
        values.append(vec)
        valids.append(ok)
        gaps.append(jnp.where(ok, reward - vec, 0.0))
    count = sum(lens[r][0:1, 0:1] for r in range(DP))
    mean = sum(jnp.sum(g, axis=1, keepdims=True) for g in gaps) / count
    centered = [jnp.where(ok, g - mean, 0.0) for ok, g in zip(valids, gaps)]
    variance = sum(jnp.sum(c * c, axis=1, keepdims=True) for c in centered) / count
    for r in range(DP):
        small[r : r + 1, :] = values[r]
        small[DP + r : DP + r + 1, :] = jnp.where(
            valids[r], centered[r] * lax.rsqrt(variance + 1e-05), 0.0
        )

    for h in range(NH):

        @pl.when(z < T - 1)
        def _(h=h):
            own_send(h, 0).wait_send()

        @pl.when(z > 0)
        def _(h=h):
            own_send(h, 1).wait_send()

    for k in range(1, T):
        for s, here, way, more in sides(k):

            @pl.when(here & more)
            def _(s=s, way=way):
                for h in range(NH):
                    tok_send(s, h, way).wait_send()

                def sent(c):
                    mx_send(c, s, way).wait_send()

                loop(C, sent)

        w_drain(k)
    for way, more in ((0, z < T - 1), (1, z > 0)):

        @pl.when(more)
        def _(way=way):
            for f in range(2):
                wz_send(z, f, way).wait_send()

            def sent(c):
                mx_send(c, z, way).wait_send()

            loop(C, sent)

    def rs_drain(c):
        for d in range(T):

            @pl.when(z < d)
            def _(d=d):
                rs_send(c, d, 0, False).wait_send()

            @pl.when(z > d)
            def _(d=d):
                rs_send(c, d, 1, False).wait_send()

    loop(C, rs_drain)

    def kv_drain(n):
        s, h = (lax.div(n, NH), lax.rem(n, NH))
        for i in range(2):
            for d in range(1, S):

                @pl.when(kv_direct(d))
                def _(d=d, i=i):
                    kv_send(d, s, h, i).wait_send()

            if square:

                @pl.when(relays(i))
                def _(i=i):
                    kv_relay_copy(s, h, i).wait_send()

    loop(T * NH, kv_drain)
    for d in range(1, T):
        fs_send(d).wait_send()
    for i, peer in enumerate(peers):
        mn_send(i, peer).wait_send()


def local(
    tokens, attn_gain, w_qkv, w_out, mlp_gain, w_up, w_down, pool_gain, pool_bias, value_weight,
    valid_frames,
):
    T, S, DP = (lax.axis_size("tensor"), lax.axis_size("seq"), lax.axis_size("dp"))
    rows, width = tokens.shape[1:]
    block = rows * T
    fr_dev = block // TOK_FRAME
    chunks = width // LANES
    hcols = w_qkv.shape[2]
    heads = hcols // HEAD_DIM
    C, NH = (CHUNKS, HALVES)
    cr = rows // C
    qc = T * cr
    NP = DP * S
    assert TOK_FRAME % rows == 0 and S * fr_dev <= LANES and DP == 2
    lens = jnp.broadcast_to(valid_frames.astype(F32)[:, None, None], (DP, chunks, LANES))
    vm = pl.BlockSpec(memory_space=pltpu.VMEM)
    hbm = pl.BlockSpec(memory_space=pl.ANY)
    dma = pltpu.SemaphoreType.DMA
    small_rows = -(-2 * DP // 8) * 8
    hidden, small = pl.pallas_call(
        kernel,
        out_shape=(
            jax.ShapeDtypeStruct((C, cr, width), BF16),
            jax.ShapeDtypeStruct((small_rows, LANES), F32),
        ),
        in_specs=[vm, vm, hbm, hbm, vm, hbm, hbm, vm, vm, vm, vm],
        out_specs=(vm, vm),
        scratch_shapes=[
            pltpu.VMEM(w_qkv.shape, BF16),
            pltpu.VMEM((T, NP, hcols // NP, width), BF16),
            pltpu.VMEM(w_up.shape, BF16),
            pltpu.VMEM(w_down.shape, BF16),
            pltpu.VMEM((T, C, cr, width), BF16),
            pltpu.VMEM((T, C, cr, hcols), BF16),
            pltpu.VMEM((S, T, NH, 2, rows // NH, hcols), BF16),
            pltpu.VMEM((heads, 1, qc), F32),
            pltpu.VMEM((heads, 1, qc), F32),
            pltpu.VMEM((heads, HEAD_DIM, qc), F32),
            pltpu.VMEM((C, T, qc, hcols), BF16),
            pltpu.VMEM((T, cr, width), BF16),
            pltpu.VMEM((C, cr, width), F32),
            pltpu.VMEM((qc, width), BF16),
            pltpu.VMEM((qc, w_up.shape[1]), BF16),
            pltpu.VMEM((C, T, cr, width), BF16),
            pltpu.VMEM((C, 2, T, cr, width), BF16),
            pltpu.VMEM((T, chunks, LANES), F32),
            pltpu.VMEM((DP, S, fr_dev, chunks, LANES), F32),
            dma((4,)),
            dma((2, T, NH)),
            dma((T, NH)),
            dma((S, T, NH, 2)),
            dma((S, T, NH, 2)),
            dma((T, NH, 2)),
            dma((2, T, 2)),
            dma((S, T, 2)),
            dma((T, 2)),
            dma((S, T, 2)),
            dma((T, NP, 2)),
            dma((2, C, T)),
            dma((C, T)),
            dma((2, C, T)),
            dma((2, C, T)),
            dma((T,)),
            dma((T,)),
            dma((DP * S,)),
            dma((DP, S)),
        ],
        compiler_params=pltpu.CompilerParams(
            collective_id=0, has_side_effects=True, vmem_limit_bytes=67043328
        ),
    )(
        tokens.reshape(C, cr, width),
        attn_gain[None],
        w_qkv,
        w_out.reshape(NP, hcols // NP, width),
        mlp_gain[None],
        w_up,
        w_down,
        pool_gain.reshape(chunks, LANES),
        pool_bias.reshape(chunks, LANES),
        value_weight.reshape(chunks, LANES),
        lens,
    )
    roll, seq = (lax.axis_index("dp"), lax.axis_index("seq"))
    values = lax.dynamic_slice(small, (roll, seq * fr_dev), (1, fr_dev))
    advantages = lax.dynamic_slice(small, (DP + roll, seq * fr_dev), (1, fr_dev))
    return (hidden.reshape(1, rows, width), values, advantages)


def solution(mesh):
    in_specs = (
        P("dp", ("seq", "tensor"), None),
        P(),
        P(None, None, "tensor"),
        P("tensor", None),
        P(),
        P(None, "tensor"),
        P("tensor", None),
        P(),
        P(),
        P(),
        P(),
    )
    out_specs = (P("dp", ("seq", "tensor"), None), P("dp", "seq"), P("dp", "seq"))
    return jax.shard_map(local, mesh=mesh, in_specs=in_specs, out_specs=out_specs, check_vma=False)
```

time: 211 us -> 166 us (0.79)
  Pallas kernels: 205 us -> 160 us
    pallas_call x1, Pallas kernels: 205 us -> 160 us  [local(): pl.pallas_call(kernel, out_shape=(jax.ShapeDtypeStruct((C, cr, width), BF...]
where the time goes in v1:
time: 166 us
  Pallas kernels  160 us (96%)
  local copies, waits for them, and re-layouts  3.91 us (2%)
    pallas_call x1, Pallas kernels, local(): pl.pallas_call(kernel, out_shape=(jax.ShapeDtypeStruct((C, cr, width), BF...  160 us

profile of v1, /device:TPU:0, one launch (start us, length us, event | category | flops | bytes accessed | tf_op | source)
XLA Modules:
  0.0 165.7 jit_solution(7493696570463645765)
XLA Ops:
  0.6 0.7 convert_element_type.3
  1.3 0.7 broadcast_in_dim.14.lens
  2.0 160.5 %shard_map.130 = (bf16[4,32,2048]{2,1,0:T(8,128)(2,1)}, f32[8,128]{1,0:T(8,128)}) custom-call(bf16[4,32,2048]{2,1,0:T(8,128)(2,1)} %bitcast.10, f32[1,2048]{1,0:T(1,128)} %bitcast.11, bf16[3,2048,512]{2,1,0:T(8,128)(2,1)} %w_qkv_h.1, bf16[8,64,2048]{2,1,0:T(8,128)(2,1)} %bitcast.8, f32[1,2048]{1,0:T(1,128)} %bitcast.12, bf16[2048,2048]{1,0:T(8,128)(2,1)} %w_up_h.1, ...), custom_call_target="tpu_custom_call" | custom-call | tf_op jit(solution)/shard_map/pallas_call | solution.py:722
  162.4 1.4 fusion
  163.8 1.9 %copy.15 = bf16[1,128,2048]{2,1,0:T(8,128)(2,1)} copy(bf16[1,128,2048]{2,1,0:T(8,128)(2,1)} %bitcast.9) | data formatting | bytes 1048576

commit v2 on v1

--- a/solution.py
+++ b/solution.py
@@ -13,6 +13,7 @@
 CHUNKS = 4
 HALVES = 2
 LAG = 2
+GROUP = 4
 MESH = pl.DeviceIdType.MESH
 F32 = jnp.float32
 BF16 = jnp.bfloat16
@@ -36,7 +37,7 @@
     value_weight, lens,
     hidden, small,
     w_qkv, w_out, w_up, w_down, ag1, query, kv, peak, total, acc, mixed, aft, own, normed,
-    upbuf, part, rs, fsum, means,
+    upbuf, part, rs, fsum, means, dots,
     wsem, ag_s, ag_r, kv_s, kv_r, kvr_s, wz_s, wp_s, wr_s, wd_s, wo_r, mx_s, mx_r, rs_s, rs_r,
     fs_s, fs_r, mn_s, mn_r,
 ):
@@ -356,7 +357,7 @@
     def _():
         w_begin()
 
-    length = lens[pl.ds(roll, 1)][0, 0:1, 0:1].astype(jnp.int32)
+    length = lens[roll]
     to_bits = math.log2(math.e) / HEAD_DIM**0.5
 
     def attend(c):
@@ -367,29 +368,38 @@
         q_frame = me * fr_dev + lax.div(q_row, TOK_FRAME)
         k_local = lax.broadcasted_iota(jnp.int32, (fr_dev, 1, qc), 0)
 
-        def against(j, carry):
-            k_frame = j * fr_dev + k_local
-            bias = jnp.where((k_frame <= q_frame) & (k_frame < length), 0.0, -1e30)
+        def against(first, count):
+            biases = []
+            for j in range(count):
+                k_frame = (first + j) * fr_dev + k_local
+                biases.append(jnp.where((k_frame <= q_frame) & (k_frame < length), 0.0, -1e30))
             for h in range(heads):
                 cols = slice(h * HEAD_DIM, (h + 1) * HEAD_DIM)
                 q = query[:, c, :, cols].reshape(qc, HEAD_DIM)
-                k = kv[j, :, :, 0, :, cols].reshape(block, HEAD_DIM)
-                v = kv[j, :, :, 1, :, cols].reshape(block, HEAD_DIM)
-                s = lax.dot_general(k, q, (((1,), (1,)), ((), ())), preferred_element_type=F32)
-                s = s.reshape(fr_dev, TOK_FRAME, qc) * to_bits + bias
-                s = s.reshape(block, qc)
-                old = peak[h]
-                new = jnp.maximum(old, jnp.max(s, axis=0, keepdims=True))
-                weights = jnp.exp2(s - new)
-                shrink = jnp.exp2(old - new)
-                peak[h] = new
-                total[h] = total[h] * shrink + jnp.sum(weights, axis=0, keepdims=True)
-                acc[h] = acc[h] * shrink + lax.dot_general(
-                    v, weights.astype(BF16), (((0,), (0,)), ((), ())), preferred_element_type=F32
-                )
-            return carry
-
-        lax.fori_loop(0, me + 1, against, 0)
+                old, norm, out = (peak[h], total[h], acc[h])
+                for j in range(count):
+                    k = kv[first + j, :, :, 0, :, cols].reshape(block, HEAD_DIM)
+                    v = kv[first + j, :, :, 1, :, cols].reshape(block, HEAD_DIM)
+                    s = lax.dot_general(k, q, (((1,), (1,)), ((), ())), preferred_element_type=F32)
+                    s = s.reshape(fr_dev, TOK_FRAME, qc) * to_bits + biases[j]
+                    s = s.reshape(block, qc)
+                    new = jnp.maximum(old, jnp.max(s, axis=0, keepdims=True))
+                    weights = jnp.exp2(s - new)
+                    shrink = jnp.exp2(old - new)
+                    old = new
+                    norm = norm * shrink + jnp.sum(weights, axis=0, keepdims=True)
+                    out = out * shrink + lax.dot_general(
+                        v, weights.astype(BF16), (((0,), (0,)), ((), ())), preferred_element_type=F32
+                    )
+                peak[h], total[h], acc[h] = (old, norm, out)
+
+        loop(lax.div(me + 1, GROUP), lambda g: against(g * GROUP, GROUP))
+        for count in range(1, GROUP):
+
+            @pl.when(lax.rem(me + 1, GROUP) == count)
+            def _(count=count):
+                against(me + 1 - count, count)
+
         for h in range(heads):
             cols = slice(h * HEAD_DIM, (h + 1) * HEAD_DIM)
             mixed[c, z, :, cols] = jnp.transpose(acc[h] / total[h]).astype(BF16)
@@ -494,71 +504,63 @@
 
         loop(width // tile, cols_of)
 
-    w_step(1)
     for n in range(T * NH - LAG, T * NH):
         kv_relay(jnp.int32(n))
+    w_step(1)
     loop(T * NH, kv_rest)
     w_step(2)
 
-    def mix(c):
-        attend(c)
-        mx_begin(c)
-
-        @pl.when(c == 0)
+    def when(cond, *steps):
+        @pl.when(cond)
         def _():
-            for k in range(3, T):
-                w_step(k)
-
-        @pl.when(c == 1)
-        def _():
-            w_spread(1)
-
-        @pl.when(c == 2)
-        def _():
-            w_spread(2)
-            w_diagonal(1)
+            for step, *args in steps:
+                step(*args)
+
+    def mix(t):
+        attend(t)
+        when(ends | (t < 1), (mx_begin, t))
+        when(t == 0, *[(w_step, k) for k in range(3, T)], (w_spread, 1))
+        when(t == 1, (w_spread, 2), (w_diagonal, 1), (mx_step, 0, 1))
+        when(jnp.logical_not(ends) & (t == 1), (mx_begin, 1))
+        when(t == 2, *[(w_spread, k) for k in range(3, T)], (w_diagonal, 2), (mx_step, 0, 2))
 
     loop(C, mix)
     for k in range(3, T):
-        w_spread(k)
-    for k in range(2, T):
+        mx_step(0, k)
         w_diagonal(k)
+    for k in range(1, T):
+        w_finish(k)
     loads[2].wait()
     loads[3].wait()
 
+    near = [p for p in passes if p[0] == 1]
+    far = [p for p in passes if p[0] > 1]
+
     def chunk(c):
-        for k in range(1, T):
-            mx_step(c, k)
-            for w, i in passes[k - 1 : k]:
-
-                @pl.when(c > 0)
-                def _(w=w, i=i):
-                    rs_pass(c - 1, w, i)
-
-        @pl.when(c == 0)
-        def _():
-            for k in range(1, T):
-                w_finish(k)
-
+        more = c + 1 < C
         project_out(c)
-        for w, i in passes[T - 1 :]:
-
-            @pl.when(c > 0)
-            def _(w=w, i=i):
-                rs_pass(c - 1, w, i)
-
+        when(c >= 2, *[(rs_pass, c - 2, *p) for p in far])
+        when(more, (mx_step, c + 1, 1))
+        when(jnp.logical_not(ends) & (c + 2 < C), (mx_begin, c + 2))
         feed_up()
+        when(more, (mx_step, c + 1, 2))
         feed_down(c)
         rs_open(c)
-
-        @pl.when(c > 0)
-        def _():
-            rs_finish(c - 1)
+        when(more, *[(mx_step, c + 1, k) for k in range(3, T)])
+        when(c >= 1, *[(rs_pass, c - 1, *p) for p in near])
 
     loop(C, chunk)
-    for w, i in passes:
-        rs_pass(C - 1, w, i)
-    rs_finish(C - 1)
+
+    def flush(c):
+        for p in far:
+            rs_pass(c, *p)
+        rs_finish(c)
+
+    loop(C - 2, rs_finish)
+    flush(C - 2)
+    for p in near:
+        rs_pass(C - 1, *p)
+    flush(C - 1)
 
     out = hidden[...].astype(F32).reshape(rows, width)
     sums = jnp.sum(out, axis=0, keepdims=True)
@@ -594,37 +596,35 @@
                     means.at[ra, sb], means.at[ra, sb], mn_s.at[0], mn_r.at[ra, sb], peers[0]
                 ).wait_recv()
 
-    lane = lax.broadcasted_iota(jnp.int32, (1, LANES), 1)
+    frames = S * fr_dev
+    row = lax.broadcasted_iota(jnp.int32, (frames, 1), 0)
     values, gaps, valids = ([], [], [])
     for r in range(DP):
         span = lens[r]
 
-        def frame(f, carry):
-            state, vec = carry
-            m = means[r, f // fr_dev, lax.rem(f, fr_dev)]
+        def frame(f, state):
+            m = means[r, lax.div(f, fr_dev), lax.rem(f, fr_dev)]
             gate = jax.nn.sigmoid(m * pool_gain[...] + pool_bias[...])
             new = gate * state + (1.0 - gate) * m
-            state = jnp.where(span > f.astype(F32), new, state)
-            dot = jnp.sum(jnp.sum(state * value_weight[...], axis=1, keepdims=True), axis=0, keepdims=True)
-            return (state, jnp.where(lane == f, dot, vec))
-
-        zero = (jnp.zeros((chunks, LANES), F32), jnp.zeros((1, LANES), F32))
-        _, vec = lax.fori_loop(0, S * fr_dev, frame, zero)
-        length_r = span[0:1].astype(jnp.int32)
-        ok = lane < length_r
-        vec = jnp.where(ok, vec, 0.0)
-        reward = jnp.sum(jnp.where(lane == length_r - 1, vec, 0.0), axis=1, keepdims=True)
+            state = jnp.where(f < span, new, state)
+            dots[r, pl.ds(f, 1)] = jnp.sum(state * value_weight[...], axis=0, keepdims=True)
+            return state
+
+        lax.fori_loop(0, frames, frame, jnp.zeros((chunks, LANES), F32), unroll=min(frames, 8))
+        ok = row < span
+        vec = jnp.where(ok, jnp.sum(dots[r], axis=1, keepdims=True), 0.0)
+        reward = jnp.sum(jnp.where(row == span - 1, vec, 0.0), axis=0, keepdims=True)
         values.append(vec)
         valids.append(ok)
         gaps.append(jnp.where(ok, reward - vec, 0.0))
-    count = sum(lens[r][0:1, 0:1] for r in range(DP))
-    mean = sum(jnp.sum(g, axis=1, keepdims=True) for g in gaps) / count
+    count = sum(lens[r] for r in range(DP)).astype(F32)
+    mean = sum(jnp.sum(g, axis=0, keepdims=True) for g in gaps) / count
     centered = [jnp.where(ok, g - mean, 0.0) for ok, g in zip(valids, gaps)]
-    variance = sum(jnp.sum(c * c, axis=1, keepdims=True) for c in centered) / count
+    variance = sum(jnp.sum(c * c, axis=0, keepdims=True) for c in centered) / count
     for r in range(DP):
-        small[r : r + 1, :] = values[r]
-        small[DP + r : DP + r + 1, :] = jnp.where(
-            valids[r], centered[r] * lax.rsqrt(variance + 1e-05), 0.0
+        small[r] = jnp.broadcast_to(values[r], (frames, LANES))
+        small[DP + r] = jnp.broadcast_to(
+            jnp.where(valids[r], centered[r] * lax.rsqrt(variance + 1e-05), 0.0), (frames, LANES)
         )
 
     for h in range(NH):
@@ -714,18 +714,17 @@
     qc = T * cr
     NP = DP * S
     assert TOK_FRAME % rows == 0 and S * fr_dev <= LANES and DP == 2
-    lens = jnp.broadcast_to(valid_frames.astype(F32)[:, None, None], (DP, chunks, LANES))
     vm = pl.BlockSpec(memory_space=pltpu.VMEM)
     hbm = pl.BlockSpec(memory_space=pl.ANY)
     dma = pltpu.SemaphoreType.DMA
-    small_rows = -(-2 * DP // 8) * 8
+    frames = S * fr_dev
     hidden, small = pl.pallas_call(
         kernel,
         out_shape=(
             jax.ShapeDtypeStruct((C, cr, width), BF16),
-            jax.ShapeDtypeStruct((small_rows, LANES), F32),
+            jax.ShapeDtypeStruct((2 * DP, frames, LANES), F32),
         ),
-        in_specs=[vm, vm, hbm, hbm, vm, hbm, hbm, vm, vm, vm, vm],
+        in_specs=[vm, vm, hbm, hbm, vm, hbm, hbm, vm, vm, vm, pl.BlockSpec(memory_space=pltpu.SMEM)],
         out_specs=(vm, vm),
         scratch_shapes=[
             pltpu.VMEM(w_qkv.shape, BF16),
@@ -747,6 +746,7 @@
             pltpu.VMEM((C, 2, T, cr, width), BF16),
             pltpu.VMEM((T, chunks, LANES), F32),
             pltpu.VMEM((DP, S, fr_dev, chunks, LANES), F32),
+            pltpu.VMEM((DP, frames, LANES), F32),
             dma((4,)),
             dma((2, T, NH)),
             dma((T, NH)),
@@ -781,11 +781,11 @@
         pool_gain.reshape(chunks, LANES),
         pool_bias.reshape(chunks, LANES),
         value_weight.reshape(chunks, LANES),
-        lens,
+        valid_frames,
     )
     roll, seq = (lax.axis_index("dp"), lax.axis_index("seq"))
-    values = lax.dynamic_slice(small, (roll, seq * fr_dev), (1, fr_dev))
-    advantages = lax.dynamic_slice(small, (DP + roll, seq * fr_dev), (1, fr_dev))
+    values = lax.dynamic_slice(small, (roll, seq * fr_dev, 0), (1, fr_dev, 1))[..., 0]
+    advantages = lax.dynamic_slice(small, (DP + roll, seq * fr_dev, 0), (1, fr_dev, 1))[..., 0]
     return (hidden.reshape(1, rows, width), values, advantages)
 
 

time: 166 us -> 146 us (0.88)
  Pallas kernels: 160 us -> 142 us
    pallas_call x1, Pallas kernels: 160 us -> 142 us  [local(): pl.pallas_call(kernel, out_shape=(jax.ShapeDtypeStruct((C, cr, width), BF...]
where the time goes in v2:
time: 146 us
  Pallas kernels  142 us (97%)
  local copies, waits for them, and re-layouts  3.24 us (2%)
    pallas_call x1, Pallas kernels, local(): pl.pallas_call(kernel, out_shape=(jax.ShapeDtypeStruct((C, cr, width), BF...  142 us

profile of v2, /device:TPU:0, one launch (start us, length us, event | category | flops | bytes accessed | tf_op | source)
XLA Modules:
  0.0 145.6 jit_solution(10435954868308641558)
XLA Ops:
  0.6 141.7 %shard_map.130 = (bf16[4,32,2048]{2,1,0:T(8,128)(2,1)}, f32[4,8,128]{2,1,0:T(8,128)}) custom-call(bf16[4,32,2048]{2,1,0:T(8,128)(2,1)} %bitcast.12, f32[1,2048]{1,0:T(1,128)} %bitcast.13, bf16[3,2048,512]{2,1,0:T(8,128)(2,1)} %w_qkv_h.1, bf16[8,64,2048]{2,1,0:T(8,128)(2,1)} %bitcast.10, f32[1,2048]{1,0:T(1,128)} %bitcast.14, bf16[2048,2048]{1,0:T(8,128)(2,1)} %w_up_h.1, ...), custom_call_target="tpu_custom_call" | custom-call | tf_op jit(solution)/shard_map/pallas_call | solution.py:721
  142.3 1.4 dynamic-slice_reduce_fusion
  143.7 1.9 %copy.15 = bf16[1,128,2048]{2,1,0:T(8,128)(2,1)} copy(bf16[1,128,2048]{2,1,0:T(8,128)(2,1)} %bitcast.11) | data formatting | bytes 1048576

commit v3 on v2

--- a/solution.py
+++ b/solution.py
@@ -12,8 +12,9 @@
 LANES = 128
 CHUNKS = 4
 HALVES = 2
-LAG = 2
+PIECES = 2
 GROUP = 4
+EARLY = 4
 MESH = pl.DeviceIdType.MESH
 F32 = jnp.float32
 BF16 = jnp.bfloat16
@@ -38,7 +39,7 @@
     hidden, small,
     w_qkv, w_out, w_up, w_down, ag1, query, kv, peak, total, acc, mixed, aft, own, normed,
     upbuf, part, rs, fsum, means, dots,
-    wsem, ag_s, ag_r, kv_s, kv_r, kvr_s, wz_s, wp_s, wr_s, wd_s, wo_r, mx_s, mx_r, rs_s, rs_r,
+    wsem, ag_s, ag_r, kv_s, kv_r, kvr_s, wz_s, wp_s, wr_s, wd_s, wo_r, wo_p, mx_s, mx_r, rs_s, rs_r,
     fs_s, fs_r, mn_s, mn_r,
 ):
     T, S, DP = (lax.axis_size("tensor"), lax.axis_size("seq"), lax.axis_size("dp"))
@@ -96,7 +97,7 @@
 
     def tok_send(s, h, way, src=None):
         ref = ag1.at[s, pl.ds(h * per_half, per_half)]
-        return zcopy(ref if src is None else src, ref, ag_s.at[way, s, h], ag_r.at[s, h], toward(way))
+        return zcopy(ref if src is None else src, ref, ag_s.at[way, s], ag_r.at[s, h], toward(way))
 
     def own_send(h, way):
         return tok_send(z, h, way, tok.at[pl.ds(h * per_half, per_half)])
@@ -125,7 +126,7 @@
         return rcopy(ref, ref, sem, kv_r.at[j, s, h, i], {"seq": to})
 
     def kv_send(d, s, h, i):
-        return kv_copy(me, s, h, i, kv_s.at[d, s, h, i], lax.rem(me + d, S))
+        return kv_copy(me, s, h, i, kv_s.at[d], lax.rem(me + d, S))
 
     def kv_direct(d):
         cond = me + d < S
@@ -142,7 +143,7 @@
         return (me == 3) | (me == 1 + i)
 
     def kv_relay_copy(s, h, i):
-        return kv_copy(relay_from, s, h, i, kvr_s.at[s, h, i], relay_to)
+        return kv_copy(relay_from, s, h, i, kvr_s.at[0], relay_to)
 
     def kv_relay(n):
         if square:
@@ -167,7 +168,7 @@
 
                 @pl.when(cond)
                 def _(i=i):
-                    kv_copy(j, s, h, i, kv_s.at[0, s, h, i], lax.rem(me + 1, S)).wait_recv()
+                    kv_copy(j, s, h, i, kv_s.at[0], lax.rem(me + 1, S)).wait_recv()
 
             return carry
 
@@ -191,12 +192,12 @@
         half = w_out.shape[2] // 2
         return w_out.at[zz, r, pl.ds(f * half, half)]
 
-    def w_copy(zz, r, f, sem, to):
-        ref = w_ref(zz, r, f)
-        return rcopy(ref, ref, sem, wo_r.at[zz, r, f], to)
+    def w_copy(zz, b, f, sem, to):
+        ref = w_ref(zz, roll * S + b, f)
+        return rcopy(ref, ref, sem, wo_r.at[zz, b, f], to)
 
     def wz_send(zz, f, way):
-        return w_copy(zz, mine, f, wz_s.at[way, zz, f], {"tensor": toward(way)})
+        return w_copy(zz, me, f, wz_s.at[way, zz], {"tensor": toward(way)})
 
     flip_x = me + 1 - 2 * lax.rem(me, 2)
     flip_y = lax.rem(me + 2, 4)
@@ -209,26 +210,31 @@
 
     def plane_sends(zz, f):
         return [
-            w_copy(zz, mine, f, wp_s.at[n, zz, f], {"seq": to})
+            w_copy(zz, me, f, wp_s.at[n], {"seq": to})
             for n, to in enumerate(plane_targets())
         ]
 
     def die_send(zz, b, f):
-        return w_copy(zz, roll * S + b, f, wd_s.at[b, zz, f], {"dp": other})
+        ref = w_ref(zz, roll * S + b, f)
+        return rcopy(ref, ref, wd_s.at[0], wo_p.at[0], {"dp": other})
+
+    def w_arrive(zz, b, f):
+        w_copy(zz, b, f, wz_s.at[0, 0], {"dp": other}).wait_recv()
 
     def w_relay(zz, axis):
         if axis == 0:
-            return w_copy(zz, roll * S + flip_x, 0, wr_s.at[zz, 0], {"seq": flip_y})
-        return w_copy(zz, roll * S + flip_y, 1, wr_s.at[zz, 1], {"seq": flip_x})
-
-    def w_begin():
+            return w_copy(zz, flip_x, 0, wr_s.at[0], {"seq": flip_y})
+        return w_copy(zz, flip_y, 1, wr_s.at[1], {"seq": flip_x})
+
+    def w_begin(early):
+        outward = 2 * z >= T
         for f in range(2):
 
-            @pl.when(z < T - 1)
+            @pl.when((z < T - 1) & ((ends | outward) == early))
             def _(f=f):
                 wz_send(z, f, 0).start()
 
-            @pl.when(z > 0)
+            @pl.when((z > 0) & ((ends | jnp.logical_not(outward)) == early))
             def _(f=f):
                 wz_send(z, f, 1).start()
 
@@ -259,7 +265,7 @@
                 if square:
                     for axis, b in ((0, flip_x), (1, flip_y)):
                         for f in range(2):
-                            die_send(zz, b, f).wait_recv()
+                            w_arrive(zz, b, f)
                         w_relay(zz, axis).start()
                         for f in range(2):
                             die_send(zz, b, f).start()
@@ -267,7 +273,7 @@
                     for d in range(1, S):
                         b = lax.rem(me + d, S)
                         for f in range(2):
-                            die_send(zz, b, f).wait_recv()
+                            w_arrive(zz, b, f)
                             die_send(zz, b, f).start()
 
     def w_diagonal(k):
@@ -277,46 +283,57 @@
                 @pl.when(here)
                 def _(zz=zz):
                     for f in range(2):
-                        copy = die_send(zz, flip_d, f)
-                        copy.wait_recv()
-                        copy.start()
-
-    def w_finish(k):
-        for zz, here, _, _ in sides(k):
-
-            @pl.when(here)
-            def _(zz=zz):
-                def piece(b, carry):
-                    for f in range(2):
-                        w_copy(
-                            zz, other * S + b, f, wd_s.at[b, zz, f], {"dp": other}
-                        ).wait_recv()
-                    return carry
-
-                lax.fori_loop(0, S, piece, 0)
-
-    def w_drain(k):
-        for zz, here, way, more in sides(k):
-
-            @pl.when(here)
-            def _(zz=zz, way=way, more=more):
-                for f in range(2):
-
-                    @pl.when(more)
-                    def _(f=f):
-                        wz_send(zz, f, way).wait_send()
-
-                    for copy in plane_sends(zz, f):
-                        copy.wait_send()
-                    if square:
-                        w_relay(zz, f).wait_send()
-
-                def piece(b, carry):
-                    for f in range(2):
-                        die_send(zz, b, f).wait_send()
-                    return carry
-
-                lax.fori_loop(0, S, piece, 0)
+                        w_arrive(zz, flip_d, f)
+                        die_send(zz, flip_d, f).start()
+
+    def w_bulk(sem_s, sem_r, ref):
+        return rcopy(ref, ref, sem_s, sem_r, {"dp": other})
+
+    def w_finish():
+        ref = w_out.at[pl.ds(0, T - 1), pl.ds(0, S)]
+        w_bulk(wd_s.at[0], wo_p.at[0], ref).wait_recv()
+
+    def w_drain():
+        first = pl.ds(0, T - 1)
+        half = w_out.shape[2] // 2
+        w_bulk(wd_s.at[0], wo_p.at[0], w_out.at[first, pl.ds(0, S)]).wait_send()
+        for n, _ in enumerate(plane_targets()):
+            w_bulk(wp_s.at[n], wo_p.at[0], w_out.at[first, 0]).wait_send()
+        if square:
+            for axis in range(2):
+                w_bulk(wr_s.at[axis], wo_p.at[0], w_out.at[first, 0, pl.ds(0, half)]).wait_send()
+        for way, more in ((0, z < T - 1), (1, z > 0)):
+            for s in range(T):
+
+                @pl.when(more & ((s <= z) if way == 0 else (s >= z)))
+                def _(s=s, way=way):
+                    ref = w_out.at[s, mine]
+                    w_bulk(wz_s.at[way, s], wo_p.at[0], ref).wait_send()
+                    ref = ag1.at[s]
+                    zcopy(ref, ref, ag_s.at[way, s], ag_r.at[0, 0], toward(way)).wait_send()
+                    ref = mixed.at[:, s]
+                    zcopy(ref, ref, mx_s.at[way, s], mx_r.at[0, 0], toward(way)).wait_send()
+
+                @pl.when((z < s) if way == 0 else (z > s))
+                def _(s=s, way=way):
+                    ref = rs.at[:, way, s]
+                    zcopy(ref, ref, rs_s.at[way, s], rs_r.at[0, 0, 0, 0], toward(way)).wait_send()
+
+        for d in range(1, S):
+
+            @pl.when(kv_direct(d))
+            def _(d=d):
+                w_bulk(kv_s.at[d], wo_p.at[0], kv.at[0]).wait_send()
+
+        if square:
+
+            @pl.when(me == 3)
+            def _():
+                w_bulk(kvr_s.at[0], wo_p.at[0], kv.at[0]).wait_send()
+
+            @pl.when((me == 1) | (me == 2))
+            def _():
+                w_bulk(kvr_s.at[0], wo_p.at[0], kv.at[0, :, :, 0]).wait_send()
 
     ag1[z] = tok[...]
     loads[0].wait()
@@ -340,22 +357,24 @@
         @pl.when(i == NH)
         def _():
             loads[1].wait()
-
-            @pl.when(ends)
-            def _():
-                w_begin()
+            w_begin(True)
+
+        lag = jnp.where(ends, 1, 2)
+
+        @pl.when(i >= lag)
+        def _():
+            kv_relay(i - lag)
 
         project(s, h)
 
-        @pl.when(i >= LAG)
-        def _():
-            kv_relay(i - LAG)
+        @pl.when(ends & (i == EARLY))
+        def _():
+            w_step(1)
+
 
     loop(T * NH, gather)
 
-    @pl.when(jnp.logical_not(ends))
-    def _():
-        w_begin()
+    w_begin(False)
 
     length = lens[roll]
     to_bits = math.log2(math.e) / HEAD_DIM**0.5
@@ -406,7 +425,7 @@
 
     def mx_send(c, s, way):
         ref = mixed.at[c, s]
-        return zcopy(ref, ref, mx_s.at[way, c, s], mx_r.at[c, s], toward(way))
+        return zcopy(ref, ref, mx_s.at[way, s], mx_r.at[c, s], toward(way))
 
     def mx_begin(c):
         @pl.when(z < T - 1)
@@ -417,10 +436,10 @@
         def _():
             mx_send(c, z, 1).start()
 
-    def mx_step(c, k):
+    def mx_step(c, k, late):
         for s, here, way, more in sides(k):
 
-            @pl.when(here)
+            @pl.when(here & (((s == 0) | (s == T - 1)) == late))
             def _(s=s, way=way, more=more):
                 copy = mx_send(c, s, way)
                 copy.wait_recv()
@@ -429,20 +448,24 @@
                 def _():
                     copy.start()
 
-    def rs_send(c, d, way, opens):
-        src = part.at[c, d] if opens else rs.at[c, way, d]
-        return zcopy(src, rs.at[c, way, d], rs_s.at[way, c, d], rs_r.at[way, c, d], toward(way))
+    def rs_send(c, d, way, e, opens=False):
+        span = pl.ds(e * (cr // PIECES), cr // PIECES)
+        dst = rs.at[c, way, d, span]
+        src = part.at[c, d, span] if opens else dst
+        return zcopy(src, dst, rs_s.at[way, d], rs_r.at[way, c, d, e], toward(way))
 
     def rs_open(c):
         for i in range(T - 1):
 
             @pl.when((z == 0) & (T - 1 - i > z))
             def _(i=i):
-                rs_send(c, T - 1 - i, 0, True).start()
+                for e in range(PIECES):
+                    rs_send(c, T - 1 - i, 0, e, True).start()
 
             @pl.when((z == T - 1) & (i < z))
             def _(i=i):
-                rs_send(c, i, 1, True).start()
+                for e in range(PIECES):
+                    rs_send(c, i, 1, e, True).start()
 
     def rs_pass(c, w, i):
         for d, way, here in (
@@ -452,22 +475,28 @@
 
             @pl.when(here)
             def _(d=d, way=way):
-                copy = rs_send(c, d, way, False)
-                copy.wait_recv()
-                rs[c, way, d] = (rs[c, way, d].astype(F32) + part[c, d].astype(F32)).astype(BF16)
-                copy.start()
+                for e in range(PIECES):
+                    span = pl.ds(e * (cr // PIECES), cr // PIECES)
+                    copy = rs_send(c, d, way, e)
+                    copy.wait_recv()
+                    rs[c, way, d, span] = (
+                        rs[c, way, d, span].astype(F32) + part[c, d, span].astype(F32)
+                    ).astype(BF16)
+                    copy.start()
 
     def rs_finish(c):
         own[c] = own[c] + part[c, z].astype(F32)
 
         @pl.when(z > 0)
         def _():
-            rs_send(c, z, 0, False).wait_recv()
+            for e in range(PIECES):
+                rs_send(c, z, 0, e).wait_recv()
             own[c] = own[c] + rs[c, 0, z].astype(F32)
 
         @pl.when(z < T - 1)
         def _():
-            rs_send(c, z, 1, False).wait_recv()
+            for e in range(PIECES):
+                rs_send(c, z, 1, e).wait_recv()
             own[c] = own[c] + rs[c, 1, z].astype(F32)
 
         hidden[c] = own[c].astype(BF16)
@@ -504,11 +533,18 @@
 
         loop(width // tile, cols_of)
 
-    for n in range(T * NH - LAG, T * NH):
-        kv_relay(jnp.int32(n))
-    w_step(1)
+    @pl.when(jnp.logical_not(ends))
+    def _():
+        kv_relay(jnp.int32(T * NH - 2))
+
+    kv_relay(jnp.int32(T * NH - 1))
+
+    @pl.when(jnp.logical_not(ends))
+    def _():
+        w_step(1)
+
+    w_step(2)
     loop(T * NH, kv_rest)
-    w_step(2)
 
     def when(cond, *steps):
         @pl.when(cond)
@@ -518,18 +554,27 @@
 
     def mix(t):
         attend(t)
-        when(ends | (t < 1), (mx_begin, t))
-        when(t == 0, *[(w_step, k) for k in range(3, T)], (w_spread, 1))
-        when(t == 1, (w_spread, 2), (w_diagonal, 1), (mx_step, 0, 1))
-        when(jnp.logical_not(ends) & (t == 1), (mx_begin, 1))
-        when(t == 2, *[(w_spread, k) for k in range(3, T)], (w_diagonal, 2), (mx_step, 0, 2))
+        when(ends | (t == 0) | (t == C - 1), (mx_begin, t))
+        when(
+            t == 1,
+            *[(w_step, k) for k in range(3, T)],
+            (w_spread, 1),
+            (mx_step, 0, 1, False),
+        )
+        when(t == 2, (w_spread, 2), (mx_step, 0, 2, False), (mx_step, 0, 1, True))
+        when(jnp.logical_not(ends) & (t > 0) & (t < C - 1), (mx_begin, t))
+        when(t == 2, (w_diagonal, 1), (mx_step, 0, 2, True))
 
     loop(C, mix)
     for k in range(3, T):
-        mx_step(0, k)
+        w_spread(k)
+    w_diagonal(2)
+    for k in range(3, T):
+        mx_step(0, k, False)
+        mx_step(0, k, True)
         w_diagonal(k)
-    for k in range(1, T):
-        w_finish(k)
+    mx_step(1, 1, False)
+    w_finish()
     loads[2].wait()
     loads[3].wait()
 
@@ -537,17 +582,18 @@
     far = [p for p in passes if p[0] > 1]
 
     def chunk(c):
-        more = c + 1 < C
+        after, later = (c + 1 < C, c + 2 < C)
         project_out(c)
         when(c >= 2, *[(rs_pass, c - 2, *p) for p in far])
-        when(more, (mx_step, c + 1, 1))
-        when(jnp.logical_not(ends) & (c + 2 < C), (mx_begin, c + 2))
         feed_up()
-        when(more, (mx_step, c + 1, 2))
+        when(c == 0, (mx_step, 1, 1, True), (mx_step, 1, 2, False))
         feed_down(c)
         rs_open(c)
-        when(more, *[(mx_step, c + 1, k) for k in range(3, T)])
+        when(after, (mx_step, c + 1, 2, True))
+        when(later, (mx_step, c + 2, 1, False), (mx_step, c + 2, 1, True), (mx_step, c + 2, 2, False))
         when(c >= 1, *[(rs_pass, c - 1, *p) for p in near])
+        for k in range(3, T):
+            when(after, (mx_step, c + 1, k, False), (mx_step, c + 1, k, True))
 
     loop(C, chunk)
 
@@ -627,71 +673,7 @@
             jnp.where(valids[r], centered[r] * lax.rsqrt(variance + 1e-05), 0.0), (frames, LANES)
         )
 
-    for h in range(NH):
-
-        @pl.when(z < T - 1)
-        def _(h=h):
-            own_send(h, 0).wait_send()
-
-        @pl.when(z > 0)
-        def _(h=h):
-            own_send(h, 1).wait_send()
-
-    for k in range(1, T):
-        for s, here, way, more in sides(k):
-
-            @pl.when(here & more)
-            def _(s=s, way=way):
-                for h in range(NH):
-                    tok_send(s, h, way).wait_send()
-
-                def sent(c):
-                    mx_send(c, s, way).wait_send()
-
-                loop(C, sent)
-
-        w_drain(k)
-    for way, more in ((0, z < T - 1), (1, z > 0)):
-
-        @pl.when(more)
-        def _(way=way):
-            for f in range(2):
-                wz_send(z, f, way).wait_send()
-
-            def sent(c):
-                mx_send(c, z, way).wait_send()
-
-            loop(C, sent)
-
-    def rs_drain(c):
-        for d in range(T):
-
-            @pl.when(z < d)
-            def _(d=d):
-                rs_send(c, d, 0, False).wait_send()
-
-            @pl.when(z > d)
-            def _(d=d):
-                rs_send(c, d, 1, False).wait_send()
-
-    loop(C, rs_drain)
-
-    def kv_drain(n):
-        s, h = (lax.div(n, NH), lax.rem(n, NH))
-        for i in range(2):
-            for d in range(1, S):
-
-                @pl.when(kv_direct(d))
-                def _(d=d, i=i):
-                    kv_send(d, s, h, i).wait_send()
-
-            if square:
-
-                @pl.when(relays(i))
-                def _(i=i):
-                    kv_relay_copy(s, h, i).wait_send()
-
-    loop(T * NH, kv_drain)
+    w_drain()
     for d in range(1, T):
         fs_send(d).wait_send()
     for i, peer in enumerate(peers):
@@ -748,20 +730,21 @@
             pltpu.VMEM((DP, S, fr_dev, chunks, LANES), F32),
             pltpu.VMEM((DP, frames, LANES), F32),
             dma((4,)),
-            dma((2, T, NH)),
+            dma((2, T)),
             dma((T, NH)),
+            dma((S,)),
             dma((S, T, NH, 2)),
-            dma((S, T, NH, 2)),
-            dma((T, NH, 2)),
-            dma((2, T, 2)),
-            dma((S, T, 2)),
-            dma((T, 2)),
-            dma((S, T, 2)),
-            dma((T, NP, 2)),
-            dma((2, C, T)),
+            dma((1,)),
+            dma((2, T)),
+            dma((S,)),
+            dma((2,)),
+            dma((1,)),
+            dma((T, S, 2)),
+            dma((1,)),
+            dma((2, T)),
             dma((C, T)),
-            dma((2, C, T)),
-            dma((2, C, T)),
+            dma((2, T)),
+            dma((2, C, T, PIECES)),
             dma((T,)),
             dma((T,)),
             dma((DP * S,)),

time: 146 us -> 136 us (0.932)
  Pallas kernels: 142 us -> 132 us
    pallas_call x1, Pallas kernels: 142 us -> 132 us  [local(): pl.pallas_call(kernel, out_shape=(jax.ShapeDtypeStruct((C, cr, width), BF...]
where the time goes in v3:
time: 136 us
  Pallas kernels  132 us (97%)
  local copies, waits for them, and re-layouts  3.24 us (2%)
    pallas_call x1, Pallas kernels, local(): pl.pallas_call(kernel, out_shape=(jax.ShapeDtypeStruct((C, cr, width), BF...  132 us

profile of v3, /device:TPU:0, one launch (start us, length us, event | category | flops | bytes accessed | tf_op | source)
XLA Modules:
  0.0 135.7 jit_solution(13006362327797949733)
XLA Ops:
  0.6 131.8 %shard_map.130 = (bf16[4,32,2048]{2,1,0:T(8,128)(2,1)}, f32[4,8,128]{2,1,0:T(8,128)}) custom-call(bf16[4,32,2048]{2,1,0:T(8,128)(2,1)} %bitcast.12, f32[1,2048]{1,0:T(1,128)} %bitcast.13, bf16[3,2048,512]{2,1,0:T(8,128)(2,1)} %w_qkv_h.1, bf16[8,64,2048]{2,1,0:T(8,128)(2,1)} %bitcast.10, f32[1,2048]{1,0:T(1,128)} %bitcast.14, bf16[2048,2048]{1,0:T(8,128)(2,1)} %w_up_h.1, ...), custom_call_target="tpu_custom_call" | custom-call | tf_op jit(solution)/shard_map/pallas_call | solution.py:703
  132.5 1.4 %dynamic-slice_reduce_fusion = (f32[2]{0:T(128)}, f32[2]{0:T(128)}) fusion(f32[4,8,128]{2,1,0:T(8,128)} %get-tuple-element.6, s32[]{:T(128)S(6)} %select_n.12, s32[]{:T(128)S(6)} %select_n.11, s32[]{:T(128)S(6)} %select_n.10), kind=kLoop, calls=%fused_computation | loop fusion | bytes 44 | tf_op jit(solution)/shard_map/dynamic_slice | solution.py:771
  133.8 1.9 %copy.15 = bf16[1,128,2048]{2,1,0:T(8,128)(2,1)} copy(bf16[1,128,2048]{2,1,0:T(8,128)(2,1)} %bitcast.11) | data formatting | bytes 1048576

commit v4 on v3

--- a/solution.py
+++ b/solution.py
@@ -34,10 +34,10 @@
 
 
 def kernel(
-    tok, attn_gain, w_qkv_h, w_out_h, mlp_gain, w_up_h, w_down_h, pool_gain, pool_bias,
-    value_weight, lens,
+    tok_h, attn_gain_h, w_qkv_h, w_out_h, mlp_gain_h, w_up_h, w_down_h, pool_gain_h, pool_bias_h,
+    value_weight_h, lens,
     hidden, small,
-    w_qkv, w_out, w_up, w_down, ag1, query, kv, peak, total, acc, mixed, aft, own, normed,
+    tok, attn_gain, mlp_gain, pool_gain, pool_bias, value_weight, w_qkv, w_out, w_up, w_down, ag1, query, kv, peak, total, acc, mixed, aft, own, normed,
     upbuf, part, rs, fsum, means, dots,
     wsem, ag_s, ag_r, kv_s, kv_r, kvr_s, wz_s, wp_s, wr_s, wd_s, wo_r, wo_p, mx_s, mx_r, rs_s, rs_r,
     fs_s, fs_r, mn_s, mn_r,
@@ -65,7 +65,11 @@
     loads = [
         pltpu.make_async_copy(src, dst, wsem.at[i])
         for i, (src, dst) in enumerate(
-            ((w_qkv_h, w_qkv), (w_out_h, w_out.at[z]), (w_up_h, w_up), (w_down_h, w_down))
+            (
+                (tok_h, tok), (attn_gain_h, attn_gain), (w_qkv_h, w_qkv), (w_out_h, w_out.at[z]),
+                (w_up_h, w_up), (w_down_h, w_down), (mlp_gain_h, mlp_gain),
+                (pool_gain_h, pool_gain), (pool_bias_h, pool_bias), (value_weight_h, value_weight),
+            )
         )
     ]
     for load in loads:
@@ -81,6 +85,7 @@
                 peers.append({"dp": lax.rem(roll + a, DP), "seq": lax.rem(me + b, S)})
     for peer in peers:
         pl.semaphore_signal(barrier, 1, device_id=peer, device_id_type=MESH)
+    loads[0].wait()
     pl.semaphore_wait(barrier, T - 1 + len(peers))
 
     def rcopy(src, dst, s_sem, r_sem, to):
@@ -263,10 +268,12 @@
             @pl.when(here)
             def _(zz=zz):
                 if square:
-                    for axis, b in ((0, flip_x), (1, flip_y)):
-                        for f in range(2):
-                            w_arrive(zz, b, f)
+                    sources = ((0, flip_x), (1, flip_y))
+                    for axis, b in sources:
+                        w_arrive(zz, b, axis)
                         w_relay(zz, axis).start()
+                    for axis, b in sources:
+                        w_arrive(zz, b, 1 - axis)
                         for f in range(2):
                             die_send(zz, b, f).start()
                 else:
@@ -336,7 +343,8 @@
                 w_bulk(kvr_s.at[0], wo_p.at[0], kv.at[0, :, :, 0]).wait_send()
 
     ag1[z] = tok[...]
-    loads[0].wait()
+    loads[1].wait()
+    loads[2].wait()
 
     def gather(i):
         u, h = (lax.div(i, NH), lax.rem(i, NH))
@@ -356,7 +364,7 @@
 
         @pl.when(i == NH)
         def _():
-            loads[1].wait()
+            loads[3].wait()
             w_begin(True)
 
         lag = jnp.where(ends, 1, 2)
@@ -574,9 +582,10 @@
         mx_step(0, k, True)
         w_diagonal(k)
     mx_step(1, 1, False)
+    mx_step(1, 1, True)
     w_finish()
-    loads[2].wait()
-    loads[3].wait()
+    for load in loads[4:]:
+        load.wait()
 
     near = [p for p in passes if p[0] == 1]
     far = [p for p in passes if p[0] > 1]
@@ -584,9 +593,9 @@
     def chunk(c):
         after, later = (c + 1 < C, c + 2 < C)
         project_out(c)
+        when(c == 0, (mx_step, 1, 2, False))
+        feed_up()
         when(c >= 2, *[(rs_pass, c - 2, *p) for p in far])
-        feed_up()
-        when(c == 0, (mx_step, 1, 1, True), (mx_step, 1, 2, False))
         feed_down(c)
         rs_open(c)
         when(after, (mx_step, c + 1, 2, True))
@@ -706,9 +715,15 @@
             jax.ShapeDtypeStruct((C, cr, width), BF16),
             jax.ShapeDtypeStruct((2 * DP, frames, LANES), F32),
         ),
-        in_specs=[vm, vm, hbm, hbm, vm, hbm, hbm, vm, vm, vm, pl.BlockSpec(memory_space=pltpu.SMEM)],
+        in_specs=[hbm] * 10 + [pl.BlockSpec(memory_space=pltpu.SMEM)],
         out_specs=(vm, vm),
         scratch_shapes=[
+            pltpu.VMEM((C, cr, width), BF16),
+            pltpu.VMEM((1, width), F32),
+            pltpu.VMEM((1, width), F32),
+            pltpu.VMEM((chunks, LANES), F32),
+            pltpu.VMEM((chunks, LANES), F32),
+            pltpu.VMEM((chunks, LANES), F32),
             pltpu.VMEM(w_qkv.shape, BF16),
             pltpu.VMEM((T, NP, hcols // NP, width), BF16),
             pltpu.VMEM(w_up.shape, BF16),
@@ -729,7 +744,7 @@
             pltpu.VMEM((T, chunks, LANES), F32),
             pltpu.VMEM((DP, S, fr_dev, chunks, LANES), F32),
             pltpu.VMEM((DP, frames, LANES), F32),
-            dma((4,)),
+            dma((10,)),
             dma((2, T)),
             dma((T, NH)),
             dma((S,)),

time: 136 us -> 134 us (0.985)
  Pallas kernels: 132 us -> 130 us
    pallas_call x1, Pallas kernels: 132 us -> 130 us  [local(): pl.pallas_call(kernel, out_shape=(jax.ShapeDtypeStruct((C, cr, width), BF...]
where the time goes in v4:
time: 134 us
  Pallas kernels  130 us (97%)
  local copies, waits for them, and re-layouts  3.24 us (2%)
    pallas_call x1, Pallas kernels, local(): pl.pallas_call(kernel, out_shape=(jax.ShapeDtypeStruct((C, cr, width), BF...  130 us

profile of v4, /device:TPU:0, one launch (start us, length us, event | category | flops | bytes accessed | tf_op | source)
XLA Modules:
  0.0 133.7 jit_solution(15907790846006205421)
XLA Ops:
  0.6 129.8 %shard_map.130 = (bf16[4,32,2048]{2,1,0:T(8,128)(2,1)}, f32[4,8,128]{2,1,0:T(8,128)}) custom-call(bf16[4,32,2048]{2,1,0:T(8,128)(2,1)} %bitcast.12, f32[1,2048]{1,0:T(1,128)} %bitcast.13, bf16[3,2048,512]{2,1,0:T(8,128)(2,1)} %w_qkv_h.1, bf16[8,64,2048]{2,1,0:T(8,128)(2,1)} %bitcast.10, f32[1,2048]{1,0:T(1,128)} %bitcast.14, bf16[2048,2048]{1,0:T(8,128)(2,1)} %w_up_h.1, ...), custom_call_target="tpu_custom_call" | custom-call | tf_op jit(solution)/shard_map/pallas_call | solution.py:712
  130.5 1.4 %dynamic-slice_reduce_fusion = (f32[2]{0:T(128)}, f32[2]{0:T(128)}) fusion(f32[4,8,128]{2,1,0:T(8,128)} %get-tuple-element.6, s32[]{:T(128)S(6)} %select_n.12, s32[]{:T(128)S(6)} %select_n.11, s32[]{:T(128)S(6)} %select_n.10), kind=kLoop, calls=%fused_computation | loop fusion | bytes 44 | tf_op jit(solution)/shard_map/dynamic_slice | solution.py:786
  131.8 1.9 %copy.15 = bf16[1,128,2048]{2,1,0:T(8,128)(2,1)} copy(bf16[1,128,2048]{2,1,0:T(8,128)(2,1)} %bitcast.11) | data formatting | bytes 1048576

commit v5 on v4

--- a/solution.py
+++ b/solution.py
@@ -126,12 +126,18 @@
         from_left = jnp.where(paired, odd, longer)
         return (jnp.where(from_left == 1, z - k, z + k), from_left)
 
-    def kv_copy(j, s, h, i, sem, to):
+    def kv_copy(j, s, h, i, sem, to, relayed):
         ref = kv.at[j, s, h, i]
-        return rcopy(ref, ref, sem, kv_r.at[j, s, h, i], {"seq": to})
+        slot = jnp.where(relayed, (s * NH + h) * 2 + i, T * NH * 2 + j)
+        return rcopy(ref, ref, sem, kv_r.at[slot], {"seq": to})
 
     def kv_send(d, s, h, i):
-        return kv_copy(me, s, h, i, kv_s.at[d], lax.rem(me + d, S))
+        relayed = me < 0
+        if square and d == 1 and i == 0:
+            relayed = me == 0
+        if square and d == 2:
+            relayed = (me == 1) | (i == 1)
+        return kv_copy(me, s, h, i, kv_s.at[d], lax.rem(me + d, S), relayed)
 
     def kv_direct(d):
         cond = me + d < S
@@ -147,8 +153,8 @@
     def relays(i):
         return (me == 3) | (me == 1 + i)
 
-    def kv_relay_copy(s, h, i):
-        return kv_copy(relay_from, s, h, i, kvr_s.at[0], relay_to)
+    def kv_relay_copy(s, h, i, arrives):
+        return kv_copy(relay_from, s, h, i, kvr_s.at[0], relay_to, (me >= 0) if arrives else (me < 0))
 
     def kv_relay(n):
         if square:
@@ -158,26 +164,21 @@
 
                 @pl.when(relays(i))
                 def _(i=i):
-                    copy = kv_relay_copy(s, h, i)
-                    copy.wait_recv()
-                    copy.start()
-
-    def kv_rest(n):
-        s, h = (lax.div(n, NH), lax.rem(n, NH))
-
-        def source(j, carry):
+                    kv_relay_copy(s, h, i, True).wait_recv()
+                    kv_relay_copy(s, h, i, False).start()
+
+    def kv_rest(j):
+        def bulk(cond, ref):
+            @pl.when((j < me) & cond)
+            def _():
+                rcopy(ref, ref, kv_s.at[0], kv_r.at[T * NH * 2 + j], {"dp": other}).wait_recv()
+
+        if square:
+            bulk(j != relay_from, kv.at[j])
             for i in range(2):
-                cond = j < me
-                if square:
-                    cond = cond & jnp.logical_not(relays(i) & (j == relay_from))
-
-                @pl.when(cond)
-                def _(i=i):
-                    kv_copy(j, s, h, i, kv_s.at[0], lax.rem(me + 1, S)).wait_recv()
-
-            return carry
-
-        lax.fori_loop(0, S - 1, source, 0)
+                bulk((j == relay_from) & (me == 1 + i), kv.at[j, :, :, 1 - i])
+        else:
+            bulk(j >= 0, kv.at[j])
 
     def project(s, h):
         floats = ag1[s, pl.ds(h * per_half, per_half)].astype(F32).reshape(hr, width)
@@ -552,7 +553,7 @@
         w_step(1)
 
     w_step(2)
-    loop(T * NH, kv_rest)
+    loop(S - 1, kv_rest)
 
     def when(cond, *steps):
         @pl.when(cond)
@@ -748,7 +749,7 @@
             dma((2, T)),
             dma((T, NH)),
             dma((S,)),
-            dma((S, T, NH, 2)),
+            dma((T * NH * 2 + S,)),
             dma((1,)),
             dma((2, T)),
             dma((S,)),

time: 134 us -> 134 us (level)
  no operation moved by 1% of the time
where the time goes in v5:
time: 134 us; the launch traced here: 133 us
  Pallas kernels  129 us (96%)
  local copies, waits for them, and re-layouts  3.24 us (2%)
    pallas_call x1, Pallas kernels, local(): pl.pallas_call(kernel, out_shape=(jax.ShapeDtypeStruct((C, cr, width), BF...  129 us

profile of v5, /device:TPU:0, one launch (start us, length us, event | category | flops | bytes accessed | tf_op | source)
XLA Modules:
  0.0 133.3 jit_solution(3827913597147937801)
XLA Ops:
  0.6 129.5 %shard_map.130 = (bf16[4,32,2048]{2,1,0:T(8,128)(2,1)}, f32[4,8,128]{2,1,0:T(8,128)}) custom-call(bf16[4,32,2048]{2,1,0:T(8,128)(2,1)} %bitcast.12, f32[1,2048]{1,0:T(1,128)} %bitcast.13, bf16[3,2048,512]{2,1,0:T(8,128)(2,1)} %w_qkv_h.1, bf16[8,64,2048]{2,1,0:T(8,128)(2,1)} %bitcast.10, f32[1,2048]{1,0:T(1,128)} %bitcast.14, bf16[2048,2048]{1,0:T(8,128)(2,1)} %w_up_h.1, ...), custom_call_target="tpu_custom_call" | custom-call | tf_op jit(solution)/shard_map/pallas_call | solution.py:713
  130.1 1.4 %dynamic-slice_reduce_fusion = (f32[2]{0:T(128)}, f32[2]{0:T(128)}) fusion(f32[4,8,128]{2,1,0:T(8,128)} %get-tuple-element.6, s32[]{:T(128)S(6)} %select_n.12, s32[]{:T(128)S(6)} %select_n.11, s32[]{:T(128)S(6)} %select_n.10), kind=kLoop, calls=%fused_computation | loop fusion | bytes 44 | tf_op jit(solution)/shard_map/dynamic_slice | solution.py:787
  131.5 1.9 %copy.15 = bf16[1,128,2048]{2,1,0:T(8,128)(2,1)} copy(bf16[1,128,2048]{2,1,0:T(8,128)(2,1)} %bitcast.11) | data formatting | bytes 1048576
